TPU v7x, 32 devices: a whole 2x2x4 slice. The times are simulated.
32 devices in a mesh: tm: 8 (over z, y), freq: 4 (over x, core).
Axes of the slice: x: 2, y: 2, z: 4, core: 2. Of those that a mesh axis runs over, the one named last changes fastest.
Arguments:
- snapshots: bfloat16 [4352, 3, 4096], P('tm', None, 'freq'), may hold values from -200 to 200
- block_starts: int32 [32], replicated, may hold values from 0 to 4032, as said below
- freq_index: int32 [16], replicated, may hold values from 0 to 128
Outputs:
- modes: bfloat16 [16, 32, 2, 3, 4096], P(None, None, None, None, ('freq', 'tm'))
- energy: float32 [16], replicated
Inputs may be any that keep to these rules, and one draw needn't show every extreme that they name: `block_starts`: block b starts at b * 128 plus between 0 and 64.
All inputs are finite; a program needn't handle non-finite values.
Results may differ from a plain program's by a relative error of at most 0.0085.
Values may be sent and summed in bfloat16 or wider, within the bound.
A program may use at most 64 MiB of HBM per device.

v0:
```python
import functools
import math

import jax
import jax.numpy as jnp
import numpy as np
from jax import lax
from jax.experimental import pallas as pl
from jax.experimental.pallas import tpu as pltpu
from jax.sharding import PartitionSpec as P

NB = 32
NFFT = 256
NF = 16
NSIT = 6


def for_sending(shard):
    return jax.tree.map(lambda a: a.astype(jnp.bfloat16) if a.dtype == jnp.float32 else a, shard)


def dft_rows(freq_index):
    times_idx = jnp.arange(NFFT, dtype=jnp.int32)
    phase_int = freq_index[:, None] * times_idx[None, :] % NFFT
    angles = 2.0 * math.pi / NFFT * phase_int.astype(jnp.float32)
    window = 0.5 - 0.5 * jnp.cos(2.0 * math.pi / NFFT * times_idx.astype(jnp.float32))
    scaling = 1.0 / jnp.sqrt(jnp.sum(window * window))
    cosine = window[None, :] * jnp.cos(angles) * scaling
    sine_rows = -window[None, :] * jnp.sin(angles) * scaling
    return jnp.stack([cosine, sine_rows], 1).reshape(2 * NF, NFFT).astype(jnp.bfloat16)


def block_rows(block_starts):
    return block_starts[:, None] + jnp.arange(NFFT, dtype=jnp.int32)[None, :]


def matmul_batch(left, right):
    return jnp.einsum("fij,fjk->fik", left, right, precision=lax.Precision.HIGHEST)


def whiten(summed, points):
    gram_re = summed[:, 0]
    gram_im = summed[:, 1]
    top_rows = jnp.concatenate([gram_re, -gram_im], 2)
    low_rows = jnp.concatenate([gram_im, gram_re], 2)
    hermit = jnp.concatenate([top_rows, low_rows], 1)
    frob = jnp.sqrt(jnp.sum(hermit * hermit, axis=(1, 2)) + 1e-06)
    identity = jnp.eye(2 * NB, dtype=jnp.float32)[None]
    iterate = hermit / frob[:, None, None]
    inverse = jnp.broadcast_to(identity, hermit.shape)
    for iteration in range(NSIT):
        factor = 1.5 * identity - 0.5 * matmul_batch(inverse, iterate)
        iterate = matmul_batch(iterate, factor)
        inverse = matmul_batch(factor, inverse)
    columns = inverse[:, :, :NB] * jnp.sqrt(6.0 * points / frob)[:, None, None]
    upper = columns[:, :NB]
    lower = columns[:, NB:]
    coefficients = jnp.stack([jnp.stack([upper, -lower], 1), jnp.stack([lower, upper], 1)], 1)
    energy = jnp.trace(gram_re, axis1=1, axis2=2) / (3.0 * NB * points)
    return (coefficients, energy)


def local(snapshots, block_starts, freq_index):
    dft_table = dft_rows(freq_index)
    offsets = block_rows(block_starts)
    series = lax.all_to_all(snapshots, "tm", split_axis=2, concat_axis=0, tiled=True)
    count = series.shape[1]
    width = series.shape[2]
    columns_all = series.reshape(series.shape[0], count * width)
    windows = jnp.take(columns_all, offsets, axis=0)
    spectra_part = jnp.einsum(
        "rt,btn->rbn", dft_table, windows, preferred_element_type=jnp.float32
    ).astype(jnp.bfloat16)
    spectra = spectra_part.reshape(2 * NF, NB, count, width)
    width = spectra.shape[3]
    points = float(width * lax.axis_size("tm") * lax.axis_size("freq"))
    flat_spec = spectra.reshape(NF, 2, NB, 3 * width)
    real_part = flat_spec[:, 0]
    imag_part = flat_spec[:, 1]
    gram_re = jnp.einsum("fbn,fcn->fbc", real_part, real_part, preferred_element_type=jnp.float32)
    gram_re = gram_re + jnp.einsum(
        "fbn,fcn->fbc", imag_part, imag_part, preferred_element_type=jnp.float32
    )
    cross_terms = jnp.einsum(
        "fbn,fcn->fbc", real_part, imag_part, preferred_element_type=jnp.float32
    )
    partial_gram = jnp.stack([gram_re, cross_terms - jnp.swapaxes(cross_terms, 1, 2)], 1)
    shared = lax.psum_scatter(partial_gram, "freq", scatter_dimension=0, tiled=True)
    shared = lax.psum(shared, "tm")
    coef_part, energy_part = whiten(shared, points)
    coefficients, energy = (
        lax.all_gather(for_sending(coef_part), "freq", axis=0, tiled=True).astype(coef_part.dtype),
        lax.all_gather(for_sending(energy_part), "freq", axis=0, tiled=True).astype(
            energy_part.dtype
        ),
    )
    coef_bf = jnp.transpose(coefficients.astype(jnp.bfloat16), (0, 4, 1, 2, 3))
    modes = jnp.einsum(
        "fjorb,frbn->fjon", coef_bf, flat_spec, preferred_element_type=jnp.float32
    ).astype(jnp.bfloat16)
    return (modes.reshape(NF, NB, 2, 3, width), energy)


MESH = pl.DeviceIdType.MESH
ROWS = 2 * NF
HOP = 128
JIT = 64


def plan(n, rows, total, width):
    if n < 2 or n % 2 or NB % n or total % (2 * NF) or width != 128 or rows % 16:
        return None
    per = NB // n
    if per < 4 or per % 2:
        return None
    slots = per + 4
    whole = [[] for _ in range(slots)]
    shared = [[] for _ in range(slots)]
    holders = []
    for block in range(NB):
        touched = [
            dev for dev in range(n)
            if HOP * block < rows * (dev + 1) and HOP * block + JIT + NFFT > rows * dev
        ]
        holders.append(touched)
        if len(touched) > 2:
            return None
        for dev in touched:
            slot = block - per * dev + 2
            if not 0 <= slot < slots:
                return None
            if len(touched) == 2:
                if (slot < slots // 2) != (dev == touched[1]):
                    return None
                shared[slot].append(dev)
            else:
                whole[slot].append(dev)
    return per, whole, shared, holders


def base_table(ints_ref):
    row = lax.broadcasted_iota(jnp.int32, (ROWS, NFFT), 0)
    times_idx = lax.broadcasted_iota(jnp.int32, (ROWS, NFFT), 1)
    freqs = jnp.zeros((ROWS, NFFT), jnp.int32)
    for f in range(NF):
        freqs = jnp.where((row >> 1) == f, ints_ref[NB + f], freqs)
    phase = (freqs * times_idx) & (NFFT - 1)
    angles = 2.0 * math.pi / NFFT * phase.astype(jnp.float32)
    window = 0.5 - 0.5 * jnp.cos(2.0 * math.pi / NFFT * times_idx.astype(jnp.float32))
    hann = 0.5 - 0.5 * np.cos(2.0 * math.pi / NFFT * np.arange(NFFT))
    scaling = np.float32(1.0 / np.sqrt(np.sum(hann * hann)))
    cosine = window * jnp.cos(angles) * scaling
    sine = -window * jnp.sin(angles) * scaling
    return jnp.where((row & 1) == 1, sine, cosine).astype(jnp.bfloat16)


def shifted(base, shift, rows):
    source = lax.broadcasted_iota(jnp.int32, (NFFT, rows), 0)
    target = lax.broadcasted_iota(jnp.int32, (NFFT, rows), 1)
    pick = jnp.where(source - target == shift, 1.0, 0.0).astype(jnp.bfloat16)
    return jnp.dot(base, pick, preferred_element_type=jnp.float32).astype(jnp.bfloat16)


def expanders(spread_ref, mask_ref):
    row = lax.broadcasted_iota(jnp.int32, (NB * 6, 2 * NB), 0)
    col = lax.broadcasted_iota(jnp.int32, (NB * 6, 2 * NB), 1)
    first = 6 * (col & (NB - 1))
    hit = (row >= first) & (row < first + 6) & ((row & 1) == jnp.where(col >= NB, 1, 0))
    spread_ref[...] = jnp.where(hit, 1.0, 0.0).astype(jnp.bfloat16)
    row = lax.broadcasted_iota(jnp.int32, (NB * 6, 6 * NB), 0)
    col = lax.broadcasted_iota(jnp.int32, (NB * 6, 6 * NB), 1)
    pair = row >> 1
    comp = pair - 3 * ((pair * 43691) >> 17)
    part = jnp.where(col >= 4 * NB, 2, jnp.where(col >= 2 * NB, 1, 0))
    mask_ref[...] = jnp.where(comp == part, 1.0, 0.0)


def member(index, devs):
    if not devs:
        return None
    if devs == list(range(devs[0], devs[-1] + 1)):
        return (index >= devs[0]) & (index <= devs[-1])
    hit = index == devs[0]
    for dev in devs[1:]:
        hit = hit | (index == dev)
    return hit


def kernel(n, nf_dev, per, whole, shared, holders, points, x_hbm, ints_hbm,
           modes_ref, energy_ref, ints_ref, t_ref, spread_ref, mask_ref, xv, parts,
           others, sendb, recvb, spec32, spec, gpart, gath, msg, crecv, load_sem, psend, precv,
           asend, arecv, gsend, grecv, csend, crcv):
    tm = lax.axis_index("tm")
    fr = lax.axis_index("freq")
    total = n * nf_dev
    lin = tm * nf_dev + fr
    step, lowest = total // (2 * NF), total // 4
    slots = per + 4
    mine = (lin - lowest) // step
    owns = (lin >= lowest) & (lin < lowest + NF * step) & ((lin - lowest) % step == 0)
    half_n = n // 2
    parity = tm % 2

    def owner(f):
        return lowest + f * step

    def where_is(index):
        return {"tm": index // nf_dev, "freq": index % nf_dev}

    small = pltpu.make_async_copy(ints_hbm, ints_ref, load_sem.at[3])
    small.start()
    for c in range(3):
        pltpu.make_async_copy(x_hbm.at[c], xv.at[c], load_sem.at[c]).start()
    barrier = pltpu.get_barrier_semaphore()

    @pl.loop(1, total)
    def _(k):
        pl.semaphore_signal(barrier, inc=1, device_id=where_is((lin + k) % total), device_id_type=MESH)

    small.wait()
    rows = xv.shape[1]
    base = base_table(ints_ref)
    for slot in range(slots):
        block = per * tm + slot - 2
        start = ints_ref[jnp.clip(block, 0, NB - 1)]
        inside = (block >= 0) & (block < NB)
        shift = jnp.where(inside, rows * tm - start, 4 * (rows + NFFT))
        t_ref[slot * ROWS : (slot + 1) * ROWS, :] = shifted(base, shift, rows)
    expanders(spread_ref, mask_ref)
    width = xv.shape[2]
    pw = width // n
    def exchange(slot):
        low = slot < slots // 2
        there = slot + per if low else slot - per
        return pltpu.make_async_remote_copy(
            src_ref=parts.at[slot, 1 - parity], dst_ref=others.at[there],
            send_sem=psend.at[slot], recv_sem=precv.at[there],
            device_id={"tm": (tm + n - 1) % n if low else (tm + 1) % n, "freq": fr},
            device_id_type=MESH)

    def arrival(slot):
        return pltpu.make_async_remote_copy(
            src_ref=parts.at[slot, 1 - parity], dst_ref=others.at[slot],
            send_sem=psend.at[slot], recv_sem=precv.at[slot],
            device_id={"tm": tm, "freq": fr}, device_id_type=MESH)

    outward = []
    for reach in range(slots // 2):
        outward += [slots // 2 + reach, slots // 2 - 1 - reach]
    inward = [slot + per if slot < slots // 2 else slot - per for slot in outward]

    def compute(first, last):
        for c in range(3):
            part = jnp.dot(t_ref[first * ROWS : last * ROWS, :], xv[c], preferred_element_type=jnp.float32)
            for slot in range(first, last):
                for dest in range(n):
                    at = dest // 2 * pw
                    parts[slot, dest % 2, c, :, at : at + pw] = part[
                        (slot - first) * ROWS : (slot - first + 1) * ROWS, dest * pw : (dest + 1) * pw]

    def send_parts(chosen):
        for slot in chosen:
            if shared[slot]:
                @pl.when(member(tm, shared[slot]))
                def _(slot=slot):
                    exchange(slot).start()

    for c in range(3):
        pltpu.make_async_copy(x_hbm.at[c], xv.at[c], load_sem.at[c]).wait()
    inner = [slot for slot in outward if 2 <= slot < slots - 2]
    compute(2, slots - 2)
    pl.semaphore_wait(barrier, total - 1)
    send_parts(inner)
    compute(0, 2)
    compute(slots - 2, slots)
    send_parts([slot for slot in outward if slot not in inner])

    def scatter(slot, dest):
        return pltpu.make_async_remote_copy(
            src_ref=sendb.at[slot, dest], dst_ref=recvb.at[per * tm + slot - 2],
            send_sem=asend.at[slot, dest], recv_sem=arecv.at[per * tm + slot - 2],
            device_id={"tm": dest, "freq": fr}, device_id_type=MESH)

    def same_side(k):
        return 2 * ((tm // 2 + k) % half_n) + parity

    def other_side(k):
        return 2 * ((tm // 2 + k) % half_n) + 1 - parity

    def finish(slot, side, add):
        for q in range(half_n):
            for c in range(3):
                at = q * pw
                value = parts[slot, side, c, :, at : at + pw]
                if add:
                    value = value + others[slot, c, :, at : at + pw]
                sendb[slot, 2 * q + side, :, c * pw : (c + 1) * pw] = value.astype(jnp.bfloat16)

    def keep(slot):
        recvb[per * tm + slot - 2] = sendb[slot, tm]

    for slot in range(slots):
        if whole[slot]:
            @pl.when(member(tm, whole[slot]))
            def _(slot=slot):
                finish(slot, parity, False)
                finish(slot, 1 - parity, False)

                @pl.loop(1, half_n)
                def _(k):
                    scatter(slot, same_side(k)).start()

                @pl.loop(0, half_n)
                def _(k):
                    scatter(slot, other_side(k)).start()

                keep(slot)

    for slot in inward:
        if shared[slot]:
            @pl.when(member(tm, shared[slot]))
            def _(slot=slot):
                arrival(slot).wait_recv()
                finish(slot, parity, True)

                @pl.loop(1, half_n)
                def _(k):
                    scatter(slot, same_side(k)).start()

                keep(slot)

    ordered = [b for b in range(NB) if len(holders[b]) == 1] + [b for b in range(NB) if len(holders[b]) == 2]
    for block in ordered:
        @pl.when(jnp.logical_not(member(tm, holders[block])))
        def _(block=block):
            pltpu.make_async_remote_copy(
                src_ref=sendb.at[0, 0], dst_ref=recvb.at[block], send_sem=asend.at[0, 0],
                recv_sem=arecv.at[block], device_id={"tm": tm, "freq": fr},
                device_id_type=MESH).wait_recv()

    for block in range(NB):
        values = recvb[block]
        for c in range(3):
            spec32[c, block * ROWS : (block + 1) * ROWS, :] = values[:, c * 128 : (c + 1) * 128].astype(jnp.float32)

    def to_owner(f):
        return pltpu.make_async_remote_copy(
            src_ref=gpart.at[f], dst_ref=gath.at[lin], send_sem=gsend.at[f],
            recv_sem=grecv.at[lin], device_id=where_is(owner(f)), device_id_type=MESH)

    for f in range(NF):
        real = [spec32[c, pl.ds(2 * f, NB, stride=ROWS), :].astype(jnp.bfloat16) for c in range(3)]
        imag = [spec32[c, pl.ds(2 * f + 1, NB, stride=ROWS), :].astype(jnp.bfloat16) for c in range(3)]
        for c in range(3):
            spec[f, c * 2 * NB : c * 2 * NB + NB, :] = real[c]
            spec[f, c * 2 * NB + NB : (c + 1) * 2 * NB, :] = imag[c]
        lhs = jnp.concatenate(real + imag, axis=1)
        rhs = jnp.concatenate([lhs, jnp.concatenate(imag + [-v for v in real], axis=1)], axis=0)
        gram = lax.dot_general(lhs, rhs, (((1,), (1,)), ((), ())), preferred_element_type=jnp.float32)
        half = NB // 2
        gpart[f] = jnp.concatenate([gram[:half], gram[half:]], axis=1)
        if f % 4 == 3:
            for sent in range(f - 3, f + 1):
                @pl.when(lin != owner(sent))
                def _(sent=sent):
                    to_owner(sent).start()

    def coef_to(index):
        return pltpu.make_async_remote_copy(
            src_ref=msg, dst_ref=crecv.at[mine], send_sem=csend.at[index],
            recv_sem=crcv.at[mine], device_id=where_is(index), device_id_type=MESH)

    @pl.when(owns)
    def _():
        gath[lin] = gpart[mine]

        @pl.loop(1, total)
        def _(k):
            src = (lin + k) % total
            pltpu.make_async_remote_copy(
                src_ref=gpart.at[0], dst_ref=gath.at[src], send_sem=gsend.at[0],
                recv_sem=grecv.at[src], device_id=where_is(src), device_id_type=MESH).wait_recv()

        packed = jnp.sum(gath[...], axis=0)
        both = jnp.concatenate([packed[:, : 2 * NB], packed[:, 2 * NB :]], axis=0)
        gram_re = both[:, :NB]
        gram_im = both[:, NB:]
        hermit = jnp.concatenate([
            jnp.concatenate([gram_re, -gram_im], axis=1),
            jnp.concatenate([gram_im, gram_re], axis=1)], axis=0)
        frob = jnp.sqrt(jnp.sum(hermit * hermit, axis=(0, 1), keepdims=True) + 1e-06)
        ri = lax.broadcasted_iota(jnp.int32, (2 * NB, 2 * NB), 0)
        ci = lax.broadcasted_iota(jnp.int32, (2 * NB, 2 * NB), 1)
        identity = jnp.where(ri == ci, 1.0, 0.0).astype(jnp.float32)
        energy = jnp.sum(jnp.where((ri == ci) & (ri < NB), hermit, 0.0), axis=(0, 1), keepdims=True) / (3.0 * NB * points)

        def mul(a, b):
            return jnp.dot(a, b, precision=lax.Precision.HIGHEST, preferred_element_type=jnp.float32)

        iterate = hermit / frob
        inverse = identity
        for step in range(NSIT):
            factor = 1.5 * identity - 0.5 * (iterate if step == 0 else mul(inverse, iterate))
            if step < NSIT - 1:
                iterate = mul(iterate, factor)
                inverse = factor if step == 0 else mul(factor, inverse)
            else:
                inverse = mul(factor[:NB], inverse)
        scaled = inverse[:NB] * jnp.sqrt(6.0 * points / frob)
        msg[:16, :] = jnp.concatenate([scaled[:16], scaled[16:]], axis=1).astype(jnp.bfloat16)
        high = energy.astype(jnp.bfloat16).astype(jnp.float32)
        lane = lax.broadcasted_iota(jnp.int32, (16, 128), 1)
        tail = jnp.where(lane == 0, high, jnp.where(lane == 1, energy - high, 0.0))
        msg[16:, :] = tail.astype(jnp.bfloat16)
        crecv[mine] = msg[...]

        @pl.loop(1, total)
        def _(k):
            coef_to((lin + k) % total).start()

    for slot in range(slots):
        if shared[slot]:
            @pl.when(member(tm, shared[slot]))
            def _(slot=slot):
                exchange(slot).wait_send()

                @pl.loop(1, half_n)
                def _(k):
                    scatter(slot, same_side(k)).wait_send()

        if whole[slot]:
            @pl.when(member(tm, whole[slot]))
            def _(slot=slot):
                @pl.loop(1, half_n)
                def _(k):
                    scatter(slot, same_side(k)).wait_send()

                @pl.loop(0, half_n)
                def _(k):
                    scatter(slot, other_side(k)).wait_send()

    for f in range(NF):
        @pl.when(lin != owner(f))
        def _(f=f):
            to_owner(f).wait_send()

    for f in range(NF):
        @pl.when(lin != owner(f))
        def _(f=f):
            pltpu.make_async_remote_copy(
                src_ref=msg, dst_ref=crecv.at[f], send_sem=csend.at[f], recv_sem=crcv.at[f],
                device_id=where_is(owner(f)), device_id_type=MESH).wait_recv()

    lanes = lax.broadcasted_iota(jnp.int32, (NB, 2 * NB), 1)
    signs = jnp.where(lanes < NB, 1.0, -1.0).astype(jnp.bfloat16)
    wide_lane = lax.broadcasted_iota(jnp.int32, (1, NF), 1)
    energies = jnp.zeros((1, NF), jnp.float32)
    for f in range(NF):
        pairs = crecv[f, :16, :]
        straight = jnp.concatenate([pairs[:, : 2 * NB], pairs[:, 2 * NB :]], axis=0)
        crossed = jnp.concatenate([straight[:, NB:], straight[:, :NB]], axis=1)
        stacked = jnp.concatenate([straight * signs, crossed], axis=0)
        tiled = jnp.concatenate([stacked] * 3, axis=1)
        full = jnp.dot(spread_ref[...], tiled, preferred_element_type=jnp.float32)
        full = (full * mask_ref[...]).astype(jnp.bfloat16)
        modes_ref[f * 6 * NB : (f + 1) * 6 * NB, :] = jnp.dot(
            full, spec[f], preferred_element_type=jnp.float32).astype(jnp.bfloat16)
        tail = crecv[f, 16:, :].astype(jnp.float32)
        energies = jnp.where(wide_lane == f, jnp.sum(tail[:1, :], axis=1, keepdims=True), energies)
    energy_ref[...] = energies

    @pl.when(owns)
    def _():
        @pl.loop(1, total)
        def _(k):
            coef_to((lin + k) % total).wait_send()


def fused(n, nf_dev, chosen, snapshots, block_starts, freq_index):
    per, whole, shared, holders = chosen
    rows, count, wide = snapshots.shape
    total = n * nf_dev
    pw = wide // n
    slots = per + 4
    f32, bf16 = jnp.float32, jnp.bfloat16
    dma = pltpu.SemaphoreType.DMA
    vmem = pl.BlockSpec(memory_space=pltpu.VMEM)
    modes, energy = pl.pallas_call(
        functools.partial(kernel, n, nf_dev, per, whole, shared, holders, float(wide * nf_dev)),
        out_shape=(jax.ShapeDtypeStruct((NF * NB * 6, pw), bf16), jax.ShapeDtypeStruct((1, NF), f32)),
        in_specs=[pl.BlockSpec(memory_space=pltpu.HBM)] * 2,
        out_specs=(vmem, vmem),
        scratch_shapes=[
            pltpu.SMEM((NB + NF,), jnp.int32),
            pltpu.VMEM((slots * ROWS, rows), bf16),
            pltpu.VMEM((NB * 6, 2 * NB), bf16),
            pltpu.VMEM((NB * 6, 6 * NB), f32),
            pltpu.VMEM((3, rows, wide), bf16),
            pltpu.VMEM((slots, 2, 3, ROWS, wide // 2), f32),
            pltpu.VMEM((slots, 3, ROWS, wide // 2), f32),
            pltpu.VMEM((slots, n, ROWS, 3 * pw), bf16),
            pltpu.VMEM((NB, ROWS, 3 * pw), bf16),
            pltpu.VMEM((3, NB * ROWS, pw), f32),
            pltpu.VMEM((NF, 6 * NB, pw), bf16),
            pltpu.VMEM((NF, NB // 2, 4 * NB), f32),
            pltpu.VMEM((total, NB // 2, 4 * NB), f32),
            pltpu.VMEM((32, 4 * NB), bf16),
            pltpu.VMEM((NF, 32, 4 * NB), bf16),
            dma((4,)), dma((slots,)), dma((slots,)), dma((slots, n)), dma((NB,)),
            dma((NF,)), dma((total,)), dma((total,)), dma((NF,)),
        ],
        compiler_params=pltpu.CompilerParams(
            collective_id=0, has_side_effects=True, vmem_limit_bytes=54_000_000),
    )(jnp.transpose(snapshots, (1, 0, 2)), jnp.concatenate([block_starts, freq_index]))
    modes = modes.reshape(NF, NB, 3, 2, pw).transpose(0, 1, 3, 2, 4)
    return modes, energy.reshape(NF)


def solution(mesh):
    n, nf_dev = mesh.shape["tm"], mesh.shape["freq"]

    def body(snapshots, block_starts, freq_index):
        rows, _, wide = snapshots.shape
        chosen = plan(n, rows, n * nf_dev, wide // n)
        if chosen is None:
            return local(snapshots, block_starts, freq_index)
        return fused(n, nf_dev, chosen, snapshots, block_starts, freq_index)

    return jax.shard_map(
        body,
        mesh=mesh,
        in_specs=(P("tm", None, "freq"), P(), P()),
        out_specs=(P(None, None, None, None, ("freq", "tm")), P()),
        check_vma=False,
    )
```

profile of v0, /device:TPU:0, one launch (start us, length us, event | category | flops | bytes accessed | tf_op | source)
XLA Modules:
  0.0 58.1 jit_solution(3537304485672514483)
XLA Ops:
  0.6 0.7 %pad_add_fusion.ints_hbm = s32[48]{0:T(128)S(1)} fusion(s32[16]{0:T(128)} %param.5, s32[32]{0:T(128)} %param.4), kind=kLoop, calls=%fused_computation | loop fusion | flops 48 | bytes 384 | tf_op jit(solution)/shard_map/concatenate | solution.py:514
  1.4 55.3 %shard_map.50 = (bf16[3072,128]{1,0:T(8,128)(2,1)S(1)}, f32[1,16]{1,0:T(1,128)S(1)}) custom-call(bf16[3,544,1024]{2,1,0:T(8,128)(2,1)} %bitcast.7, s32[48]{0:T(128)S(1)} %pad_add_fusion.ints_hbm), custom_call_target="tpu_custom_call" | custom-call | tf_op jit(solution)/shard_map/pallas_call | solution.py:488
  56.7 0.9 %copy.7 = bf16[16,32,2,3,128]{4,2,3,1,0:T(2,128)(2,1)} copy(bf16[16,32,2,3,128]{4,2,3,1,0:T(2,128)(2,1)S(1)} %bitcast.5) | data formatting | bytes 1572864
  57.6 0.5 copy.8
where the time goes:
time: 58.2 us; the launch traced here: 58.1 us
  Pallas kernels  55.3 us (95%)
  local copies, waits for them, and re-layouts  1.39 us (2%)
  other arithmetic  0.75 us (1%)
  between operations  0.64 us (1%)
    pallas_call x1, Pallas kernels, fused(): pl.pallas_call(functools.partial(kernel, n, nf_dev, per, whole, shared, h...  55.3 us
    unnamed x2, local copies, waits for them, and re-layouts  1.39 us

commit v1 on v0

--- a/solution.py
+++ b/solution.py
@@ -138,12 +138,12 @@
     return per, whole, shared, holders
 
 
-def base_table(ints_ref):
+def base_table(freqs_ref):
     row = lax.broadcasted_iota(jnp.int32, (ROWS, NFFT), 0)
     times_idx = lax.broadcasted_iota(jnp.int32, (ROWS, NFFT), 1)
     freqs = jnp.zeros((ROWS, NFFT), jnp.int32)
     for f in range(NF):
-        freqs = jnp.where((row >> 1) == f, ints_ref[NB + f], freqs)
+        freqs = jnp.where((row >> 1) == f, freqs_ref[f], freqs)
     phase = (freqs * times_idx) & (NFFT - 1)
     angles = 2.0 * math.pi / NFFT * phase.astype(jnp.float32)
     window = 0.5 - 0.5 * jnp.cos(2.0 * math.pi / NFFT * times_idx.astype(jnp.float32))
@@ -186,10 +186,10 @@
     return hit
 
 
-def kernel(n, nf_dev, per, whole, shared, holders, points, x_hbm, ints_hbm,
-           modes_ref, energy_ref, ints_ref, t_ref, spread_ref, mask_ref, xv, parts,
-           others, sendb, recvb, spec32, spec, gpart, gath, msg, crecv, load_sem, psend, precv,
-           asend, arecv, gsend, grecv, csend, crcv):
+def kernel(n, nf_dev, per, whole, shared, holders, points, x_hbm, starts_hbm, freqs_hbm,
+           modes_ref, energy_ref, starts_ref, freqs_ref, t_ref, spread_ref, mask_ref, xv, parts,
+           others, sendb, recvb, spec32, spec, gpart, gath, msg, crecv, emsg, erecv, load_sem,
+           psend, precv, asend, arecv, gsend, grecv, csend, crcv, esend, ercv):
     tm = lax.axis_index("tm")
     fr = lax.axis_index("freq")
     total = n * nf_dev
@@ -207,8 +207,10 @@
     def where_is(index):
         return {"tm": index // nf_dev, "freq": index % nf_dev}
 
-    small = pltpu.make_async_copy(ints_hbm, ints_ref, load_sem.at[3])
+    small = pltpu.make_async_copy(freqs_hbm, freqs_ref, load_sem.at[3])
     small.start()
+    starts = pltpu.make_async_copy(starts_hbm, starts_ref, load_sem.at[4])
+    starts.start()
     for c in range(3):
         pltpu.make_async_copy(x_hbm.at[c], xv.at[c], load_sem.at[c]).start()
     barrier = pltpu.get_barrier_semaphore()
@@ -219,10 +221,11 @@
 
     small.wait()
     rows = xv.shape[1]
-    base = base_table(ints_ref)
+    base = base_table(freqs_ref)
+    starts.wait()
     for slot in range(slots):
         block = per * tm + slot - 2
-        start = ints_ref[jnp.clip(block, 0, NB - 1)]
+        start = starts_ref[jnp.clip(block, 0, NB - 1)]
         inside = (block >= 0) & (block < NB)
         shift = jnp.where(inside, rows * tm - start, 4 * (rows + NFFT))
         t_ref[slot * ROWS : (slot + 1) * ROWS, :] = shifted(base, shift, rows)
@@ -348,6 +351,7 @@
             src_ref=gpart.at[f], dst_ref=gath.at[lin], send_sem=gsend.at[f],
             recv_sem=grecv.at[lin], device_id=where_is(owner(f)), device_id_type=MESH)
 
+    upper = lax.broadcasted_iota(jnp.int32, (NB, NB), 1) >= lax.broadcasted_iota(jnp.int32, (NB, NB), 0)
     for f in range(NF):
         real = [spec32[c, pl.ds(2 * f, NB, stride=ROWS), :].astype(jnp.bfloat16) for c in range(3)]
         imag = [spec32[c, pl.ds(2 * f + 1, NB, stride=ROWS), :].astype(jnp.bfloat16) for c in range(3)]
@@ -357,8 +361,8 @@
         lhs = jnp.concatenate(real + imag, axis=1)
         rhs = jnp.concatenate([lhs, jnp.concatenate(imag + [-v for v in real], axis=1)], axis=0)
         gram = lax.dot_general(lhs, rhs, (((1,), (1,)), ((), ())), preferred_element_type=jnp.float32)
-        half = NB // 2
-        gpart[f] = jnp.concatenate([gram[:half], gram[half:]], axis=1)
+        packed = jnp.where(upper, gram[:, :NB], gram[:, NB:])
+        gpart[f] = jnp.concatenate([packed[8 * q : 8 * q + 8] for q in range(NB // 8)], axis=1)
         if f % 4 == 3:
             for sent in range(f - 3, f + 1):
                 @pl.when(lin != owner(sent))
@@ -369,6 +373,11 @@
         return pltpu.make_async_remote_copy(
             src_ref=msg, dst_ref=crecv.at[mine], send_sem=csend.at[index],
             recv_sem=crcv.at[mine], device_id=where_is(index), device_id_type=MESH)
+
+    def energy_to(index):
+        return pltpu.make_async_remote_copy(
+            src_ref=emsg, dst_ref=erecv.at[mine], send_sem=esend.at[index],
+            recv_sem=ercv.at[mine], device_id=where_is(index), device_id_type=MESH)
 
     @pl.when(owns)
     def _():
@@ -382,36 +391,57 @@
                 recv_sem=grecv.at[src], device_id=where_is(src), device_id_type=MESH).wait_recv()
 
         packed = jnp.sum(gath[...], axis=0)
-        both = jnp.concatenate([packed[:, : 2 * NB], packed[:, 2 * NB :]], axis=0)
-        gram_re = both[:, :NB]
-        gram_im = both[:, NB:]
+        square = jnp.concatenate([packed[:, q * NB : (q + 1) * NB] for q in range(NB // 8)], axis=0)
+        flipped = jnp.transpose(square)
+        ri = lax.broadcasted_iota(jnp.int32, (NB, NB), 0)
+        ci = lax.broadcasted_iota(jnp.int32, (NB, NB), 1)
+        gram_re = jnp.where(ci >= ri, square, flipped)
+        gram_im = jnp.where(ci < ri, square, jnp.where(ci > ri, -flipped, 0.0))
+        energy = jnp.sum(jnp.where(ri == ci, gram_re, 0.0), axis=(0, 1), keepdims=True) / (3.0 * NB * points)
+        emsg[...] = jnp.broadcast_to(energy, (1, 4 * NB))
+        erecv[mine] = emsg[...]
+
+        @pl.loop(1, total)
+        def _(k):
+            energy_to((lin + k) % total).start()
+
         hermit = jnp.concatenate([
-            jnp.concatenate([gram_re, -gram_im], axis=1),
-            jnp.concatenate([gram_im, gram_re], axis=1)], axis=0)
-        frob = jnp.sqrt(jnp.sum(hermit * hermit, axis=(0, 1), keepdims=True) + 1e-06)
-        ri = lax.broadcasted_iota(jnp.int32, (2 * NB, 2 * NB), 0)
-        ci = lax.broadcasted_iota(jnp.int32, (2 * NB, 2 * NB), 1)
-        identity = jnp.where(ri == ci, 1.0, 0.0).astype(jnp.float32)
-        energy = jnp.sum(jnp.where((ri == ci) & (ri < NB), hermit, 0.0), axis=(0, 1), keepdims=True) / (3.0 * NB * points)
+            jnp.concatenate([gram_re, -gram_im, gram_re, -gram_im], axis=1),
+            jnp.concatenate([gram_im, gram_re, gram_im, gram_re], axis=1)], axis=0)
+        frob = jnp.sqrt(0.5 * jnp.sum(hermit * hermit, axis=(0, 1), keepdims=True) + 1e-06)
+        ri = lax.broadcasted_iota(jnp.int32, (2 * NB, 4 * NB), 0)
+        ci = lax.broadcasted_iota(jnp.int32, (2 * NB, 4 * NB), 1)
+        left = ci < 2 * NB
+        identity = jnp.where(ri == (ci & (2 * NB - 1)), 1.0, 0.0).astype(jnp.float32)
+
+        def pieces(a):
+            high = a.astype(jnp.bfloat16)
+            rest = a - high.astype(jnp.float32)
+            mid = rest.astype(jnp.bfloat16)
+            return high, mid, (rest - mid.astype(jnp.float32)).astype(jnp.bfloat16)
 
         def mul(a, b):
-            return jnp.dot(a, b, precision=lax.Precision.HIGHEST, preferred_element_type=jnp.float32)
+            ah, am, al = a
+            bh, bm, bl = b
+            lhs = jnp.concatenate([ah, am, jnp.where(left[: ah.shape[0]], ah, al)], axis=1)
+            rhs = jnp.concatenate([bh, bm, bh, bm, bl, bh], axis=0)
+            return jnp.dot(lhs, rhs, preferred_element_type=jnp.float32)
 
         iterate = hermit / frob
         inverse = identity
         for step in range(NSIT):
-            factor = 1.5 * identity - 0.5 * (iterate if step == 0 else mul(inverse, iterate))
+            it = pieces(iterate)
+            if step:
+                inv = pieces(inverse)
+            factor = 1.5 * identity - 0.5 * (mul(inv, it) if step else iterate)
+            fac = pieces(factor)
             if step < NSIT - 1:
-                iterate = mul(iterate, factor)
-                inverse = factor if step == 0 else mul(factor, inverse)
+                iterate = mul(it, fac)
+                inverse = mul(fac, inv) if step else factor
             else:
-                inverse = mul(factor[:NB], inverse)
-        scaled = inverse[:NB] * jnp.sqrt(6.0 * points / frob)
-        msg[:16, :] = jnp.concatenate([scaled[:16], scaled[16:]], axis=1).astype(jnp.bfloat16)
-        high = energy.astype(jnp.bfloat16).astype(jnp.float32)
-        lane = lax.broadcasted_iota(jnp.int32, (16, 128), 1)
-        tail = jnp.where(lane == 0, high, jnp.where(lane == 1, energy - high, 0.0))
-        msg[16:, :] = tail.astype(jnp.bfloat16)
+                inverse = mul(tuple(piece[:NB] for piece in fac), inv)
+        scaled = inverse * jnp.sqrt(6.0 * points / frob)
+        msg[...] = jnp.where(left[: NB // 2], scaled[: NB // 2], scaled[NB // 2 :]).astype(jnp.bfloat16)
         crecv[mine] = msg[...]
 
         @pl.loop(1, total)
@@ -450,13 +480,16 @@
             pltpu.make_async_remote_copy(
                 src_ref=msg, dst_ref=crecv.at[f], send_sem=csend.at[f], recv_sem=crcv.at[f],
                 device_id=where_is(owner(f)), device_id_type=MESH).wait_recv()
+            pltpu.make_async_remote_copy(
+                src_ref=emsg, dst_ref=erecv.at[f], send_sem=esend.at[f], recv_sem=ercv.at[f],
+                device_id=where_is(owner(f)), device_id_type=MESH).wait_recv()
 
     lanes = lax.broadcasted_iota(jnp.int32, (NB, 2 * NB), 1)
     signs = jnp.where(lanes < NB, 1.0, -1.0).astype(jnp.bfloat16)
     wide_lane = lax.broadcasted_iota(jnp.int32, (1, NF), 1)
     energies = jnp.zeros((1, NF), jnp.float32)
     for f in range(NF):
-        pairs = crecv[f, :16, :]
+        pairs = crecv[f]
         straight = jnp.concatenate([pairs[:, : 2 * NB], pairs[:, 2 * NB :]], axis=0)
         crossed = jnp.concatenate([straight[:, NB:], straight[:, :NB]], axis=1)
         stacked = jnp.concatenate([straight * signs, crossed], axis=0)
@@ -465,8 +498,7 @@
         full = (full * mask_ref[...]).astype(jnp.bfloat16)
         modes_ref[f * 6 * NB : (f + 1) * 6 * NB, :] = jnp.dot(
             full, spec[f], preferred_element_type=jnp.float32).astype(jnp.bfloat16)
-        tail = crecv[f, 16:, :].astype(jnp.float32)
-        energies = jnp.where(wide_lane == f, jnp.sum(tail[:1, :], axis=1, keepdims=True), energies)
+        energies = jnp.where(wide_lane == f, erecv[f, :, :NF], energies)
     energy_ref[...] = energies
 
     @pl.when(owns)
@@ -474,6 +506,7 @@
         @pl.loop(1, total)
         def _(k):
             coef_to((lin + k) % total).wait_send()
+            energy_to((lin + k) % total).wait_send()
 
 
 def fused(n, nf_dev, chosen, snapshots, block_starts, freq_index):
@@ -488,10 +521,11 @@
     modes, energy = pl.pallas_call(
         functools.partial(kernel, n, nf_dev, per, whole, shared, holders, float(wide * nf_dev)),
         out_shape=(jax.ShapeDtypeStruct((NF * NB * 6, pw), bf16), jax.ShapeDtypeStruct((1, NF), f32)),
-        in_specs=[pl.BlockSpec(memory_space=pltpu.HBM)] * 2,
+        in_specs=[pl.BlockSpec(memory_space=pltpu.HBM)] * 3,
         out_specs=(vmem, vmem),
         scratch_shapes=[
-            pltpu.SMEM((NB + NF,), jnp.int32),
+            pltpu.SMEM((NB,), jnp.int32),
+            pltpu.SMEM((NF,), jnp.int32),
             pltpu.VMEM((slots * ROWS, rows), bf16),
             pltpu.VMEM((NB * 6, 2 * NB), bf16),
             pltpu.VMEM((NB * 6, 6 * NB), f32),
@@ -502,16 +536,18 @@
             pltpu.VMEM((NB, ROWS, 3 * pw), bf16),
             pltpu.VMEM((3, NB * ROWS, pw), f32),
             pltpu.VMEM((NF, 6 * NB, pw), bf16),
-            pltpu.VMEM((NF, NB // 2, 4 * NB), f32),
-            pltpu.VMEM((total, NB // 2, 4 * NB), f32),
-            pltpu.VMEM((32, 4 * NB), bf16),
-            pltpu.VMEM((NF, 32, 4 * NB), bf16),
-            dma((4,)), dma((slots,)), dma((slots,)), dma((slots, n)), dma((NB,)),
-            dma((NF,)), dma((total,)), dma((total,)), dma((NF,)),
+            pltpu.VMEM((NF, NB // 4, 4 * NB), f32),
+            pltpu.VMEM((total, NB // 4, 4 * NB), f32),
+            pltpu.VMEM((NB // 2, 4 * NB), bf16),
+            pltpu.VMEM((NF, NB // 2, 4 * NB), bf16),
+            pltpu.VMEM((1, 4 * NB), f32),
+            pltpu.VMEM((NF, 1, 4 * NB), f32),
+            dma((5,)), dma((slots,)), dma((slots,)), dma((slots, n)), dma((NB,)),
+            dma((NF,)), dma((total,)), dma((total,)), dma((NF,)), dma((total,)), dma((NF,)),
         ],
         compiler_params=pltpu.CompilerParams(
             collective_id=0, has_side_effects=True, vmem_limit_bytes=54_000_000),
-    )(jnp.transpose(snapshots, (1, 0, 2)), jnp.concatenate([block_starts, freq_index]))
+    )(jnp.transpose(snapshots, (1, 0, 2)), block_starts, freq_index)
     modes = modes.reshape(NF, NB, 3, 2, pw).transpose(0, 1, 3, 2, 4)
     return modes, energy.reshape(NF)
 

time: 58.2 us -> 59.7 us (1.026)
  local copies, waits for them, and re-layouts: 1.39 us -> 2.7 us
  Pallas kernels: 55.3 us -> 56.1 us
  other arithmetic: 0.75 us -> 0 us
    unnamed x2 -> x6, local copies, waits for them, and re-layouts: 1.39 us -> 2.7 us
    pallas_call x1, Pallas kernels: 55.3 us -> 56.1 us  [fused(): pl.pallas_call(functools.partial(kernel, n, nf_dev, per, whole, shared, h...]
    concatenate x1 -> x0, other arithmetic: 0.75 us -> none  [fused(): jnp.concatenate([block_starts, freq_index])]
where the time goes in v1:
time: 59.7 us; the launch traced here: 59.5 us
  Pallas kernels  56.1 us (94%)
  local copies, waits for them, and re-layouts  2.7 us (5%)
  between operations  0.65 us (1%)
    pallas_call x1, Pallas kernels, fused(): pl.pallas_call(functools.partial(kernel, n, nf_dev, per, whole, shared, h...  56.1 us
    unnamed x6, local copies, waits for them, and re-layouts  2.7 us

profile of v1, /device:TPU:0, one launch (start us, length us, event | category | flops | bytes accessed | tf_op | source)
XLA Modules:
  0.0 59.5 jit_solution(18434815489178133625)
XLA Ops:
  0.6 0.0 copy-start
  0.6 0.6 %copy-done = s32[32]{0:T(128)S(1)} copy-done((s32[32]{0:T(128)S(1)}, s32[32]{0:T(128)}, u32[]{:S(2)}) %copy-start) | copy-done | bytes 152
  1.3 0.0 copy-start.1
  1.3 0.7 %copy-done.1 = s32[16]{0:T(128)S(1)} copy-done((s32[16]{0:T(128)S(1)}, s32[16]{0:T(128)}, u32[]{:S(2)}) %copy-start.1) | copy-done | bytes 88
  1.9 56.1 %shard_map.50 = (bf16[3072,128]{1,0:T(8,128)(2,1)S(1)}, f32[1,16]{1,0:T(1,128)S(1)}) custom-call(bf16[3,544,1024]{2,1,0:T(8,128)(2,1)} %bitcast.7, s32[32]{0:T(128)S(1)} %copy-done, s32[16]{0:T(128)S(1)} %copy-done.1), custom_call_target="tpu_custom_call" | custom-call | tf_op jit(solution)/shard_map/pallas_call | solution.py:521
  58.1 0.9 %copy.7 = bf16[16,32,2,3,128]{4,2,3,1,0:T(2,128)(2,1)} copy(bf16[16,32,2,3,128]{4,2,3,1,0:T(2,128)(2,1)S(1)} %bitcast.5) | data formatting | bytes 1572864
  59.0 0.5 copy.8
Async XLA Ops:
  0.6 0.7 %copy-start = (s32[32]{0:T(128)S(1)}, s32[32]{0:T(128)}, u32[]{:S(2)}) copy-start(s32[32]{0:T(128)} %starts_hbm.1) | copy-start | bytes 388
  1.3 0.7 %copy-start.1 = (s32[16]{0:T(128)S(1)}, s32[16]{0:T(128)}, u32[]{:S(2)}) copy-start(s32[16]{0:T(128)} %freqs_hbm.1) | copy-start | bytes 196

commit v2 on v1

--- a/solution.py
+++ b/solution.py
@@ -188,18 +188,21 @@
 
 def kernel(n, nf_dev, per, whole, shared, holders, points, x_hbm, starts_hbm, freqs_hbm,
            modes_ref, energy_ref, starts_ref, freqs_ref, t_ref, spread_ref, mask_ref, xv, parts,
-           others, sendb, recvb, spec32, spec, gpart, gath, msg, crecv, emsg, erecv, load_sem,
-           psend, precv, asend, arecv, gsend, grecv, csend, crcv, esend, ercv):
+           sendp, others, scales, oscales, sendb, recvb, spec32, spec, gpart, gath, msg, crecv,
+           load_sem, psend, precv, ssend, srecv, asend, arecv, gsend, grecv, csend, crcv):
     tm = lax.axis_index("tm")
     fr = lax.axis_index("freq")
     total = n * nf_dev
     lin = tm * nf_dev + fr
     step, lowest = total // (2 * NF), total // 4
     slots = per + 4
+    half_slots = slots // 2
     mine = (lin - lowest) // step
     owns = (lin >= lowest) & (lin < lowest + NF * step) & ((lin - lowest) % step == 0)
     half_n = n // 2
     parity = tm % 2
+    rows = xv.shape[2]
+    pw = xv.shape[3] // 2
 
     def owner(f):
         return lowest + f * step
@@ -207,12 +210,21 @@
     def where_is(index):
         return {"tm": index // nf_dev, "freq": index % nf_dev}
 
-    small = pltpu.make_async_copy(freqs_hbm, freqs_ref, load_sem.at[3])
+    def group(k):
+        return jnp.where(tm < half_n, half_n - 1 - k, k)
+
+    def load(g, c):
+        return pltpu.make_async_copy(
+            x_hbm.at[c, :, pl.ds(pl.multiple_of(g * 2 * pw, 2 * pw), 2 * pw)], xv.at[g, c],
+            load_sem.at[2 + 3 * g + c])
+
+    small = pltpu.make_async_copy(freqs_hbm, freqs_ref, load_sem.at[0])
     small.start()
-    starts = pltpu.make_async_copy(starts_hbm, starts_ref, load_sem.at[4])
+    starts = pltpu.make_async_copy(starts_hbm, starts_ref, load_sem.at[1])
     starts.start()
-    for c in range(3):
-        pltpu.make_async_copy(x_hbm.at[c], xv.at[c], load_sem.at[c]).start()
+    for k in range(half_n):
+        for c in range(3):
+            load(group(k), c).start()
     barrier = pltpu.get_barrier_semaphore()
 
     @pl.loop(1, total)
@@ -220,7 +232,6 @@
         pl.semaphore_signal(barrier, inc=1, device_id=where_is((lin + k) % total), device_id_type=MESH)
 
     small.wait()
-    rows = xv.shape[1]
     base = base_table(freqs_ref)
     starts.wait()
     for slot in range(slots):
@@ -229,54 +240,50 @@
         inside = (block >= 0) & (block < NB)
         shift = jnp.where(inside, rows * tm - start, 4 * (rows + NFFT))
         t_ref[slot * ROWS : (slot + 1) * ROWS, :] = shifted(base, shift, rows)
+    scales[...] = jnp.zeros_like(scales)
     expanders(spread_ref, mask_ref)
-    width = xv.shape[2]
-    pw = width // n
-    def exchange(slot):
-        low = slot < slots // 2
-        there = slot + per if low else slot - per
+
+    def low(slot):
+        return slot < half_slots
+
+    def pick(flag, yes, no):
+        return (yes if flag else no) if isinstance(flag, bool) else jnp.where(flag, yes, no)
+
+    def partner(slot):
+        return pick(low(slot), (tm + n - 1) % n, (tm + 1) % n)
+
+    def across(slot):
+        return pick(low(slot), slot + per, slot - per)
+
+    def is_shared(slot):
+        block = per * tm + slot - 2
+        edge = rows * (tm + pick(low(slot), 0, 1))
+        inside = (block >= 0) & (block < NB) & (edge > 0) & (edge < rows * n)
+        return inside & (HOP * block < edge) & (HOP * block + JIT + NFFT > edge)
+
+    def is_theirs(slot, dest):
+        middle = tm + pick(low(slot), 0, 1) == half_n
+        by_half = (dest < half_n) != (tm < half_n)
+        return (middle & by_half) | (jnp.logical_not(middle) & (dest % 2 != parity))
+
+    def exchange(slot, dest):
         return pltpu.make_async_remote_copy(
-            src_ref=parts.at[slot, 1 - parity], dst_ref=others.at[there],
-            send_sem=psend.at[slot], recv_sem=precv.at[there],
-            device_id={"tm": (tm + n - 1) % n if low else (tm + 1) % n, "freq": fr},
+            src_ref=sendp.at[slot, dest], dst_ref=others.at[across(slot), dest],
+            send_sem=psend.at[slot, dest], recv_sem=precv.at[across(slot), dest],
+            device_id={"tm": partner(slot), "freq": fr}, device_id_type=MESH)
+
+    def arrival(slot, dest):
+        return pltpu.make_async_remote_copy(
+            src_ref=sendp.at[slot, dest], dst_ref=others.at[slot, dest],
+            send_sem=psend.at[slot, dest], recv_sem=precv.at[slot, dest],
+            device_id={"tm": partner(slot), "freq": fr}, device_id_type=MESH)
+
+    def scale_copy(side):
+        return pltpu.make_async_remote_copy(
+            src_ref=scales.at[side], dst_ref=oscales.at[1 - side],
+            send_sem=ssend.at[side], recv_sem=srecv.at[1 - side],
+            device_id={"tm": (tm + 1) % n if side else (tm + n - 1) % n, "freq": fr},
             device_id_type=MESH)
-
-    def arrival(slot):
-        return pltpu.make_async_remote_copy(
-            src_ref=parts.at[slot, 1 - parity], dst_ref=others.at[slot],
-            send_sem=psend.at[slot], recv_sem=precv.at[slot],
-            device_id={"tm": tm, "freq": fr}, device_id_type=MESH)
-
-    outward = []
-    for reach in range(slots // 2):
-        outward += [slots // 2 + reach, slots // 2 - 1 - reach]
-    inward = [slot + per if slot < slots // 2 else slot - per for slot in outward]
-
-    def compute(first, last):
-        for c in range(3):
-            part = jnp.dot(t_ref[first * ROWS : last * ROWS, :], xv[c], preferred_element_type=jnp.float32)
-            for slot in range(first, last):
-                for dest in range(n):
-                    at = dest // 2 * pw
-                    parts[slot, dest % 2, c, :, at : at + pw] = part[
-                        (slot - first) * ROWS : (slot - first + 1) * ROWS, dest * pw : (dest + 1) * pw]
-
-    def send_parts(chosen):
-        for slot in chosen:
-            if shared[slot]:
-                @pl.when(member(tm, shared[slot]))
-                def _(slot=slot):
-                    exchange(slot).start()
-
-    for c in range(3):
-        pltpu.make_async_copy(x_hbm.at[c], xv.at[c], load_sem.at[c]).wait()
-    inner = [slot for slot in outward if 2 <= slot < slots - 2]
-    compute(2, slots - 2)
-    pl.semaphore_wait(barrier, total - 1)
-    send_parts(inner)
-    compute(0, 2)
-    compute(slots - 2, slots)
-    send_parts([slot for slot in outward if slot not in inner])
 
     def scatter(slot, dest):
         return pltpu.make_async_remote_copy(
@@ -284,53 +291,90 @@
             send_sem=asend.at[slot, dest], recv_sem=arecv.at[per * tm + slot - 2],
             device_id={"tm": dest, "freq": fr}, device_id_type=MESH)
 
-    def same_side(k):
-        return 2 * ((tm // 2 + k) % half_n) + parity
-
-    def other_side(k):
-        return 2 * ((tm // 2 + k) % half_n) + 1 - parity
-
-    def finish(slot, side, add):
-        for q in range(half_n):
-            for c in range(3):
-                at = q * pw
-                value = parts[slot, side, c, :, at : at + pw]
-                if add:
-                    value = value + others[slot, c, :, at : at + pw]
-                sendb[slot, 2 * q + side, :, c * pw : (c + 1) * pw] = value.astype(jnp.bfloat16)
-
-    def keep(slot):
-        recvb[per * tm + slot - 2] = sendb[slot, tm]
-
-    for slot in range(slots):
-        if whole[slot]:
-            @pl.when(member(tm, whole[slot]))
-            def _(slot=slot):
-                finish(slot, parity, False)
-                finish(slot, 1 - parity, False)
-
-                @pl.loop(1, half_n)
-                def _(k):
-                    scatter(slot, same_side(k)).start()
-
-                @pl.loop(0, half_n)
-                def _(k):
-                    scatter(slot, other_side(k)).start()
-
-                keep(slot)
-
-    for slot in inward:
-        if shared[slot]:
-            @pl.when(member(tm, shared[slot]))
-            def _(slot=slot):
-                arrival(slot).wait_recv()
-                finish(slot, parity, True)
-
-                @pl.loop(1, half_n)
-                def _(k):
-                    scatter(slot, same_side(k)).start()
-
-                keep(slot)
+    def deliver(slot, dest, value):
+        value = value.astype(jnp.bfloat16)
+
+        @pl.when(dest == tm)
+        def _():
+            recvb[per * tm + slot - 2] = value
+
+        @pl.when(dest != tm)
+        def _():
+            sendb[slot, dest] = value
+            scatter(slot, dest).start()
+
+    diagonal = (lax.broadcasted_iota(jnp.int32, (ROWS, 128), 0)
+                == lax.broadcasted_iota(jnp.int32, (ROWS, 128), 1))
+
+    def encode(slot, dest):
+        value = parts[dest, slot * ROWS : (slot + 1) * ROWS, :]
+        peak = jnp.maximum(jnp.max(jnp.abs(value), axis=1, keepdims=True), 1e-30)
+        whole_numbers = (value * (32767.0 / peak) + 12582912.0) - 12582912.0
+        sendp[slot, dest] = whole_numbers.astype(jnp.int32).astype(jnp.int16)
+        line = jnp.sum(jnp.where(diagonal, peak, 0.0), axis=0, keepdims=True)
+        scales[slot // half_slots, pl.ds(slot % half_slots * n + dest, 1), :] = line
+        exchange(slot, dest).start()
+
+    @pl.loop(0, half_n)
+    def _(k):
+        g = group(k)
+        for c in range(3):
+            load(g, c).wait()
+            part = jnp.dot(t_ref[...], xv[g, c], preferred_element_type=jnp.float32)
+            for d in range(2):
+                parts[2 * g + d, :, c * pw : (c + 1) * pw] = part[:, d * pw : (d + 1) * pw]
+
+        @pl.when(k == 0)
+        def _():
+            pl.semaphore_wait(barrier, total - 1)
+
+        for d in range(2):
+            for slot in range(slots):
+                if shared[slot]:
+                    @pl.when(member(tm, shared[slot]) & is_theirs(slot, 2 * g + d))
+                    def _(slot=slot, d=d):
+                        encode(slot, 2 * g + d)
+
+        for d in range(2):
+            for slot in range(slots):
+                if whole[slot]:
+                    @pl.when(member(tm, whole[slot]))
+                    def _(slot=slot, d=d):
+                        deliver(slot, 2 * g + d, parts[2 * g + d, slot * ROWS : (slot + 1) * ROWS, :])
+
+    @pl.when(tm > 0)
+    def _():
+        scale_copy(0).start()
+
+    @pl.when(tm < n - 1)
+    def _():
+        scale_copy(1).start()
+
+    @pl.when(tm > 0)
+    def _():
+        scale_copy(1).wait_recv()
+
+    @pl.when(tm < n - 1)
+    def _():
+        scale_copy(0).wait_recv()
+
+    @pl.loop(0, half_n)
+    def _(k):
+        g = group(k)
+
+        @pl.loop(0, slots)
+        def _(turn):
+            slot = (turn + half_slots * (1 - parity)) % slots
+            for d in range(2):
+                @pl.when(is_shared(slot) & jnp.logical_not(is_theirs(slot, 2 * g + d)))
+                def _(d=d):
+                    dest = 2 * g + d
+                    arrival(slot, dest).wait_recv()
+                    line = oscales[slot // half_slots, pl.ds(slot % half_slots * n + dest, 1), :]
+                    peak = jnp.sum(jnp.where(diagonal, line, 0.0), axis=1, keepdims=True)
+                    other = others[slot, dest].astype(jnp.int32).astype(jnp.float32)
+                    here = parts[dest, pl.ds(pl.multiple_of(slot * ROWS, ROWS), ROWS), :]
+                    deliver(slot, dest, here + other * (peak * (1.0 / 32767.0)))
 
     ordered = [b for b in range(NB) if len(holders[b]) == 1] + [b for b in range(NB) if len(holders[b]) == 2]
     for block in ordered:
@@ -341,10 +385,11 @@
                 recv_sem=arecv.at[block], device_id={"tm": tm, "freq": fr},
                 device_id_type=MESH).wait_recv()
 
+    pitch = spec32.shape[1] // NB
     for block in range(NB):
         values = recvb[block]
         for c in range(3):
-            spec32[c, block * ROWS : (block + 1) * ROWS, :] = values[:, c * 128 : (c + 1) * 128].astype(jnp.float32)
+            spec32[c, block * pitch : block * pitch + ROWS, :] = values[:, c * 128 : (c + 1) * 128].astype(jnp.float32)
 
     def to_owner(f):
         return pltpu.make_async_remote_copy(
@@ -353,8 +398,8 @@
 
     upper = lax.broadcasted_iota(jnp.int32, (NB, NB), 1) >= lax.broadcasted_iota(jnp.int32, (NB, NB), 0)
     for f in range(NF):
-        real = [spec32[c, pl.ds(2 * f, NB, stride=ROWS), :].astype(jnp.bfloat16) for c in range(3)]
-        imag = [spec32[c, pl.ds(2 * f + 1, NB, stride=ROWS), :].astype(jnp.bfloat16) for c in range(3)]
+        real = [spec32[c, pl.ds(2 * f, NB, stride=pitch), :].astype(jnp.bfloat16) for c in range(3)]
+        imag = [spec32[c, pl.ds(2 * f + 1, NB, stride=pitch), :].astype(jnp.bfloat16) for c in range(3)]
         for c in range(3):
             spec[f, c * 2 * NB : c * 2 * NB + NB, :] = real[c]
             spec[f, c * 2 * NB + NB : (c + 1) * 2 * NB, :] = imag[c]
@@ -369,15 +414,13 @@
                 def _(sent=sent):
                     to_owner(sent).start()
 
-    def coef_to(index):
+    def coef_to(away):
+        row, col = tm + away // nf_dev, fr + away % nf_dev
+        where = {"tm": jnp.where(row >= n, row - n, row),
+                 "freq": jnp.where(col >= nf_dev, col - nf_dev, col)}
         return pltpu.make_async_remote_copy(
-            src_ref=msg, dst_ref=crecv.at[mine], send_sem=csend.at[index],
-            recv_sem=crcv.at[mine], device_id=where_is(index), device_id_type=MESH)
-
-    def energy_to(index):
-        return pltpu.make_async_remote_copy(
-            src_ref=emsg, dst_ref=erecv.at[mine], send_sem=esend.at[index],
-            recv_sem=ercv.at[mine], device_id=where_is(index), device_id_type=MESH)
+            src_ref=msg, dst_ref=crecv.at[mine], send_sem=csend.at[away],
+            recv_sem=crcv.at[mine], device_id=where, device_id_type=MESH)
 
     @pl.when(owns)
     def _():
@@ -398,13 +441,6 @@
         gram_re = jnp.where(ci >= ri, square, flipped)
         gram_im = jnp.where(ci < ri, square, jnp.where(ci > ri, -flipped, 0.0))
         energy = jnp.sum(jnp.where(ri == ci, gram_re, 0.0), axis=(0, 1), keepdims=True) / (3.0 * NB * points)
-        emsg[...] = jnp.broadcast_to(energy, (1, 4 * NB))
-        erecv[mine] = emsg[...]
-
-        @pl.loop(1, total)
-        def _(k):
-            energy_to((lin + k) % total).start()
-
         hermit = jnp.concatenate([
             jnp.concatenate([gram_re, -gram_im, gram_re, -gram_im], axis=1),
             jnp.concatenate([gram_im, gram_re, gram_im, gram_re], axis=1)], axis=0)
@@ -441,33 +477,42 @@
             else:
                 inverse = mul(tuple(piece[:NB] for piece in fac), inv)
         scaled = inverse * jnp.sqrt(6.0 * points / frob)
+        high, mid, rest = [piece.astype(jnp.float32) for piece in pieces(energy)]
+        top = ri[:NB]
+        extra = jnp.where(top == 0, high, jnp.where(top == 1, mid, jnp.where(top == 2, rest, 0.0)))
+        scaled = jnp.where((ci[:NB] & (2 * NB - 1)) == NB + top, extra, scaled)
         msg[...] = jnp.where(left[: NB // 2], scaled[: NB // 2], scaled[NB // 2 :]).astype(jnp.bfloat16)
         crecv[mine] = msg[...]
 
-        @pl.loop(1, total)
-        def _(k):
-            coef_to((lin + k) % total).start()
-
-    for slot in range(slots):
-        if shared[slot]:
-            @pl.when(member(tm, shared[slot]))
-            def _(slot=slot):
-                exchange(slot).wait_send()
-
-                @pl.loop(1, half_n)
-                def _(k):
-                    scatter(slot, same_side(k)).wait_send()
-
-        if whole[slot]:
-            @pl.when(member(tm, whole[slot]))
-            def _(slot=slot):
-                @pl.loop(1, half_n)
-                def _(k):
-                    scatter(slot, same_side(k)).wait_send()
-
-                @pl.loop(0, half_n)
-                def _(k):
-                    scatter(slot, other_side(k)).wait_send()
+        for away in range(total - 1, 0, -1):
+            coef_to(away).start()
+
+    @pl.loop(0, slots)
+    def _(slot):
+        sharing = is_shared(slot)
+        block = per * tm + slot - 2
+        inside = (block >= 0) & (block < NB)
+        alone = inside & (HOP * block >= rows * tm) & (HOP * block + JIT + NFFT <= rows * (tm + 1))
+
+        @pl.loop(0, n)
+        def _(dest):
+            theirs = is_theirs(slot, dest)
+
+            @pl.when(sharing & theirs)
+            def _():
+                exchange(slot, dest).wait_send()
+
+            @pl.when((alone | (sharing & jnp.logical_not(theirs))) & (dest != tm))
+            def _():
+                scatter(slot, dest).wait_send()
+
+    @pl.when(tm > 0)
+    def _():
+        scale_copy(0).wait_send()
+
+    @pl.when(tm < n - 1)
+    def _():
+        scale_copy(1).wait_send()
 
     for f in range(NF):
         @pl.when(lin != owner(f))
@@ -480,17 +525,18 @@
             pltpu.make_async_remote_copy(
                 src_ref=msg, dst_ref=crecv.at[f], send_sem=csend.at[f], recv_sem=crcv.at[f],
                 device_id=where_is(owner(f)), device_id_type=MESH).wait_recv()
-            pltpu.make_async_remote_copy(
-                src_ref=emsg, dst_ref=erecv.at[f], send_sem=esend.at[f], recv_sem=ercv.at[f],
-                device_id=where_is(owner(f)), device_id_type=MESH).wait_recv()
 
     lanes = lax.broadcasted_iota(jnp.int32, (NB, 2 * NB), 1)
     signs = jnp.where(lanes < NB, 1.0, -1.0).astype(jnp.bfloat16)
+    hidden = lanes == NB + lax.broadcasted_iota(jnp.int32, (NB, 2 * NB), 0)
     wide_lane = lax.broadcasted_iota(jnp.int32, (1, NF), 1)
     energies = jnp.zeros((1, NF), jnp.float32)
     for f in range(NF):
         pairs = crecv[f]
         straight = jnp.concatenate([pairs[:, : 2 * NB], pairs[:, 2 * NB :]], axis=0)
+        found = jnp.sum(jnp.where(hidden, straight.astype(jnp.float32), 0.0), axis=(0, 1), keepdims=True)
+        energies = jnp.where(wide_lane == f, found, energies)
+        straight = jnp.where(hidden, jnp.zeros_like(straight), straight)
         crossed = jnp.concatenate([straight[:, NB:], straight[:, :NB]], axis=1)
         stacked = jnp.concatenate([straight * signs, crossed], axis=0)
         tiled = jnp.concatenate([stacked] * 3, axis=1)
@@ -498,15 +544,12 @@
         full = (full * mask_ref[...]).astype(jnp.bfloat16)
         modes_ref[f * 6 * NB : (f + 1) * 6 * NB, :] = jnp.dot(
             full, spec[f], preferred_element_type=jnp.float32).astype(jnp.bfloat16)
-        energies = jnp.where(wide_lane == f, erecv[f, :, :NF], energies)
     energy_ref[...] = energies
 
     @pl.when(owns)
     def _():
-        @pl.loop(1, total)
-        def _(k):
-            coef_to((lin + k) % total).wait_send()
-            energy_to((lin + k) % total).wait_send()
+        for away in range(total - 1, 0, -1):
+            coef_to(away).wait_send()
 
 
 def fused(n, nf_dev, chosen, snapshots, block_starts, freq_index):
@@ -529,21 +572,22 @@
             pltpu.VMEM((slots * ROWS, rows), bf16),
             pltpu.VMEM((NB * 6, 2 * NB), bf16),
             pltpu.VMEM((NB * 6, 6 * NB), f32),
-            pltpu.VMEM((3, rows, wide), bf16),
-            pltpu.VMEM((slots, 2, 3, ROWS, wide // 2), f32),
-            pltpu.VMEM((slots, 3, ROWS, wide // 2), f32),
+            pltpu.VMEM((n // 2, 3, rows, 2 * pw), bf16),
+            pltpu.VMEM((n, slots * ROWS, 3 * pw), f32),
+            pltpu.VMEM((slots, n, ROWS, 3 * pw), jnp.int16),
+            pltpu.VMEM((slots, n, ROWS, 3 * pw), jnp.int16),
+            pltpu.VMEM((2, slots // 2 * n, 128), f32),
+            pltpu.VMEM((2, slots // 2 * n, 128), f32),
             pltpu.VMEM((slots, n, ROWS, 3 * pw), bf16),
             pltpu.VMEM((NB, ROWS, 3 * pw), bf16),
-            pltpu.VMEM((3, NB * ROWS, pw), f32),
+            pltpu.VMEM((3, NB * (ROWS + 8), pw), f32),
             pltpu.VMEM((NF, 6 * NB, pw), bf16),
             pltpu.VMEM((NF, NB // 4, 4 * NB), f32),
             pltpu.VMEM((total, NB // 4, 4 * NB), f32),
             pltpu.VMEM((NB // 2, 4 * NB), bf16),
             pltpu.VMEM((NF, NB // 2, 4 * NB), bf16),
-            pltpu.VMEM((1, 4 * NB), f32),
-            pltpu.VMEM((NF, 1, 4 * NB), f32),
-            dma((5,)), dma((slots,)), dma((slots,)), dma((slots, n)), dma((NB,)),
-            dma((NF,)), dma((total,)), dma((total,)), dma((NF,)), dma((total,)), dma((NF,)),
+            dma((2 + 3 * n // 2,)), dma((slots, n)), dma((slots, n)), dma((2,)), dma((2,)),
+            dma((slots, n)), dma((NB,)), dma((NF,)), dma((total,)), dma((total,)), dma((NF,)),
         ],
         compiler_params=pltpu.CompilerParams(
             collective_id=0, has_side_effects=True, vmem_limit_bytes=54_000_000),

time: 59.7 us -> 54.5 us (0.913)
  Pallas kernels: 56.1 us -> 51 us
    pallas_call x1, Pallas kernels: 56.1 us -> 51 us  [fused(): pl.pallas_call(functools.partial(kernel, n, nf_dev, per, whole, shared, h...]
where the time goes in v2:
time: 54.5 us; the launch traced here: 54.3 us
  Pallas kernels  51 us (94%)
  local copies, waits for them, and re-layouts  2.7 us (5%)
  between operations  0.65 us (1%)
    pallas_call x1, Pallas kernels, fused(): pl.pallas_call(functools.partial(kernel, n, nf_dev, per, whole, shared, h...  51 us
    unnamed x6, local copies, waits for them, and re-layouts  2.7 us

profile of v2, /device:TPU:0, one launch (start us, length us, event | category | flops | bytes accessed | tf_op | source)
XLA Modules:
  0.0 54.3 jit_solution(7879514135243448059)
XLA Ops:
  0.6 0.0 copy-start
  0.6 0.6 %copy-done = s32[32]{0:T(128)S(1)} copy-done((s32[32]{0:T(128)S(1)}, s32[32]{0:T(128)}, u32[]{:S(2)}) %copy-start) | copy-done | bytes 152
  1.3 0.0 copy-start.1
  1.3 0.7 %copy-done.1 = s32[16]{0:T(128)S(1)} copy-done((s32[16]{0:T(128)S(1)}, s32[16]{0:T(128)}, u32[]{:S(2)}) %copy-start.1) | copy-done | bytes 88
  1.9 51.0 %shard_map.50 = (bf16[3072,128]{1,0:T(8,128)(2,1)S(1)}, f32[1,16]{1,0:T(1,128)S(1)}) custom-call(bf16[3,544,1024]{2,1,0:T(8,128)(2,1)} %bitcast.7, s32[32]{0:T(128)S(1)} %copy-done, s32[16]{0:T(128)S(1)} %copy-done.1), custom_call_target="tpu_custom_call" | custom-call | tf_op jit(solution)/shard_map/pallas_call | solution.py:564
  52.9 0.9 %copy.7 = bf16[16,32,2,3,128]{4,2,3,1,0:T(2,128)(2,1)} copy(bf16[16,32,2,3,128]{4,2,3,1,0:T(2,128)(2,1)S(1)} %bitcast.5) | data formatting | bytes 1572864
  53.8 0.5 copy.8
Async XLA Ops:
  0.6 0.7 %copy-start = (s32[32]{0:T(128)S(1)}, s32[32]{0:T(128)}, u32[]{:S(2)}) copy-start(s32[32]{0:T(128)} %starts_hbm.1) | copy-start | bytes 388
  1.3 0.7 %copy-start.1 = (s32[16]{0:T(128)S(1)}, s32[16]{0:T(128)}, u32[]{:S(2)}) copy-start(s32[16]{0:T(128)} %freqs_hbm.1) | copy-start | bytes 196

commit v3 on v2

--- a/solution.py
+++ b/solution.py
@@ -216,7 +216,7 @@
     def load(g, c):
         return pltpu.make_async_copy(
             x_hbm.at[c, :, pl.ds(pl.multiple_of(g * 2 * pw, 2 * pw), 2 * pw)], xv.at[g, c],
-            load_sem.at[2 + 3 * g + c])
+            load_sem.at[2 + g])
 
     small = pltpu.make_async_copy(freqs_hbm, freqs_ref, load_sem.at[0])
     small.start()
@@ -268,28 +268,39 @@
 
     def exchange(slot, dest):
         return pltpu.make_async_remote_copy(
-            src_ref=sendp.at[slot, dest], dst_ref=others.at[across(slot), dest],
-            send_sem=psend.at[slot, dest], recv_sem=precv.at[across(slot), dest],
+            src_ref=sendp.at[slot * n + dest], dst_ref=others.at[across(slot) * n + dest],
+            send_sem=psend.at[0], recv_sem=precv.at[across(slot) // half_slots * half_n + dest // 2],
             device_id={"tm": partner(slot), "freq": fr}, device_id_type=MESH)
 
-    def arrival(slot, dest):
+    def scale_copy(side, g):
         return pltpu.make_async_remote_copy(
-            src_ref=sendp.at[slot, dest], dst_ref=others.at[slot, dest],
-            send_sem=psend.at[slot, dest], recv_sem=precv.at[slot, dest],
-            device_id={"tm": partner(slot), "freq": fr}, device_id_type=MESH)
-
-    def scale_copy(side):
-        return pltpu.make_async_remote_copy(
-            src_ref=scales.at[side], dst_ref=oscales.at[1 - side],
-            send_sem=ssend.at[side], recv_sem=srecv.at[1 - side],
-            device_id={"tm": (tm + 1) % n if side else (tm + n - 1) % n, "freq": fr},
-            device_id_type=MESH)
+            src_ref=scales.at[side * half_n + g], dst_ref=oscales.at[(1 - side) * half_n + g],
+            send_sem=ssend.at[0], recv_sem=srecv.at[(1 - side) * half_n + g],
+            device_id={"tm": partner(side * half_slots), "freq": fr}, device_id_type=MESH)
 
     def scatter(slot, dest):
         return pltpu.make_async_remote_copy(
-            src_ref=sendb.at[slot, dest], dst_ref=recvb.at[per * tm + slot - 2],
-            send_sem=asend.at[slot, dest], recv_sem=arecv.at[per * tm + slot - 2],
+            src_ref=sendb.at[slot * n + dest], dst_ref=recvb.at[per * tm + slot - 2],
+            send_sem=asend.at[0], recv_sem=arecv.at[0],
             device_id={"tm": dest, "freq": fr}, device_id_type=MESH)
+
+    def settle(ref, sem):
+        pltpu.make_async_copy(ref, ref, sem).wait()
+
+    def settle_count(ref, count, sem, options):
+        for option in sorted(set(options)):
+            @pl.when(count == option)
+            def _(option=option):
+                settle(ref.at[pl.ds(0, option)], sem)
+
+    def edge_exists(side):
+        return pick(side == 0, tm > 0, tm < n - 1)
+
+    def at_middle(side):
+        return tm + side == half_n
+
+    def sharing(side):
+        return sum(jnp.where(is_shared(side * half_slots + k), 1, 0) for k in range(half_slots))
 
     def deliver(slot, dest, value):
         value = value.astype(jnp.bfloat16)
@@ -300,26 +311,26 @@
 
         @pl.when(dest != tm)
         def _():
-            sendb[slot, dest] = value
+            sendb[slot * n + dest] = value
             scatter(slot, dest).start()
 
     diagonal = (lax.broadcasted_iota(jnp.int32, (ROWS, 128), 0)
                 == lax.broadcasted_iota(jnp.int32, (ROWS, 128), 1))
 
-    def encode(slot, dest):
-        value = parts[dest, slot * ROWS : (slot + 1) * ROWS, :]
+    def encode(slot, g, d):
+        value = parts[2 * g + d, slot * ROWS : (slot + 1) * ROWS, :]
         peak = jnp.maximum(jnp.max(jnp.abs(value), axis=1, keepdims=True), 1e-30)
         whole_numbers = (value * (32767.0 / peak) + 12582912.0) - 12582912.0
-        sendp[slot, dest] = whole_numbers.astype(jnp.int32).astype(jnp.int16)
+        sendp[slot * n + 2 * g + d] = whole_numbers.astype(jnp.int32).astype(jnp.int16)
         line = jnp.sum(jnp.where(diagonal, peak, 0.0), axis=0, keepdims=True)
-        scales[slot // half_slots, pl.ds(slot % half_slots * n + dest, 1), :] = line
-        exchange(slot, dest).start()
+        row = 2 * (slot % half_slots) + d
+        scales[slot // half_slots * half_n + g, row : row + 1, :] = line
 
     @pl.loop(0, half_n)
     def _(k):
         g = group(k)
+        settle(xv.at[g], load_sem.at[2 + g])
         for c in range(3):
-            load(g, c).wait()
             part = jnp.dot(t_ref[...], xv[g, c], preferred_element_type=jnp.float32)
             for d in range(2):
                 parts[2 * g + d, :, c * pw : (c + 1) * pw] = part[:, d * pw : (d + 1) * pw]
@@ -333,7 +344,19 @@
                 if shared[slot]:
                     @pl.when(member(tm, shared[slot]) & is_theirs(slot, 2 * g + d))
                     def _(slot=slot, d=d):
-                        encode(slot, 2 * g + d)
+                        encode(slot, g, d)
+
+        for side in range(2):
+            @pl.when(edge_exists(side) & (jnp.logical_not(at_middle(side)) | is_theirs(side * half_slots, 2 * g)))
+            def _(side=side):
+                scale_copy(side, g).start()
+
+        for d in range(2):
+            for slot in range(slots):
+                if shared[slot]:
+                    @pl.when(member(tm, shared[slot]) & is_theirs(slot, 2 * g + d))
+                    def _(slot=slot, d=d):
+                        exchange(slot, 2 * g + d).start()
 
         for d in range(2):
             for slot in range(slots):
@@ -342,48 +365,41 @@
                     def _(slot=slot, d=d):
                         deliver(slot, 2 * g + d, parts[2 * g + d, slot * ROWS : (slot + 1) * ROWS, :])
 
-    @pl.when(tm > 0)
-    def _():
-        scale_copy(0).start()
-
-    @pl.when(tm < n - 1)
-    def _():
-        scale_copy(1).start()
-
-    @pl.when(tm > 0)
-    def _():
-        scale_copy(1).wait_recv()
-
-    @pl.when(tm < n - 1)
-    def _():
-        scale_copy(0).wait_recv()
-
-    @pl.loop(0, half_n)
-    def _(k):
-        g = group(k)
-
-        @pl.loop(0, slots)
-        def _(turn):
-            slot = (turn + half_slots * (1 - parity)) % slots
-            for d in range(2):
-                @pl.when(is_shared(slot) & jnp.logical_not(is_theirs(slot, 2 * g + d)))
-                def _(d=d):
+    counts = [sum(tm_at in devs for devs in shared) for tm_at in range(n)]
+
+    @pl.loop(0, 2)
+    def _(turn):
+        side = jnp.where(turn == 0, 1 - parity, parity)
+
+        @pl.loop(0, half_n)
+        def _(k):
+            g = group(k)
+            middle = at_middle(side)
+
+            @pl.when(edge_exists(side) & (jnp.logical_not(middle) | jnp.logical_not(is_theirs(side * half_slots, 2 * g))))
+            def _():
+                settle(oscales.at[side * half_n + g], srecv.at[side * half_n + g])
+                settle_count(others, sharing(side) * jnp.where(middle, 2, 1), precv.at[side * half_n + g],
+                             [count * twice for count in range(1, half_slots + 1) for twice in (1, 2)])
+                for d in range(2):
                     dest = 2 * g + d
-                    arrival(slot, dest).wait_recv()
-                    line = oscales[slot // half_slots, pl.ds(slot % half_slots * n + dest, 1), :]
-                    peak = jnp.sum(jnp.where(diagonal, line, 0.0), axis=1, keepdims=True)
-                    other = others[slot, dest].astype(jnp.int32).astype(jnp.float32)
-                    here = parts[dest, pl.ds(pl.multiple_of(slot * ROWS, ROWS), ROWS), :]
-                    deliver(slot, dest, here + other * (peak * (1.0 / 32767.0)))
-
-    ordered = [b for b in range(NB) if len(holders[b]) == 1] + [b for b in range(NB) if len(holders[b]) == 2]
-    for block in ordered:
-        @pl.when(jnp.logical_not(member(tm, holders[block])))
-        def _(block=block):
-            pltpu.make_async_remote_copy(
-                src_ref=sendb.at[0, 0], dst_ref=recvb.at[block], send_sem=asend.at[0, 0],
-                recv_sem=arecv.at[block], device_id={"tm": tm, "freq": fr},
-                device_id_type=MESH).wait_recv()
+                    for index in range(half_slots):
+                        slot = side * half_slots + index
+
+                        @pl.when(is_shared(slot) & jnp.logical_not(is_theirs(slot, dest)))
+                        def _(slot=slot, dest=dest, row=2 * index + d):
+                            line = oscales[side * half_n + g, row : row + 1, :]
+                            peak = jnp.sum(jnp.where(diagonal, line, 0.0), axis=1, keepdims=True)
+                            other = others[slot * n + dest].astype(jnp.int32).astype(jnp.float32)
+                            here = parts[dest, pl.ds(pl.multiple_of(slot * ROWS, ROWS), ROWS), :]
+                            deliver(slot, dest, here + other * (peak * (1.0 / 32767.0)))
+
+
+    alone = [sum(tm_at in devs for devs in whole) for tm_at in range(n)]
+    for tm_at in range(n):
+        @pl.when(tm == tm_at)
+        def _(tm_at=tm_at):
+            settle(recvb.at[pl.ds(0, NB - alone[tm_at] - counts[tm_at])], arecv.at[0])
 
     pitch = spec32.shape[1] // NB
     for block in range(NB):
@@ -393,8 +409,8 @@
 
     def to_owner(f):
         return pltpu.make_async_remote_copy(
-            src_ref=gpart.at[f], dst_ref=gath.at[lin], send_sem=gsend.at[f],
-            recv_sem=grecv.at[lin], device_id=where_is(owner(f)), device_id_type=MESH)
+            src_ref=gpart.at[f], dst_ref=gath.at[lin], send_sem=gsend.at[0],
+            recv_sem=grecv.at[0], device_id=where_is(owner(f)), device_id_type=MESH)
 
     upper = lax.broadcasted_iota(jnp.int32, (NB, NB), 1) >= lax.broadcasted_iota(jnp.int32, (NB, NB), 0)
     for f in range(NF):
@@ -419,20 +435,14 @@
         where = {"tm": jnp.where(row >= n, row - n, row),
                  "freq": jnp.where(col >= nf_dev, col - nf_dev, col)}
         return pltpu.make_async_remote_copy(
-            src_ref=msg, dst_ref=crecv.at[mine], send_sem=csend.at[away],
-            recv_sem=crcv.at[mine], device_id=where, device_id_type=MESH)
+            src_ref=msg, dst_ref=crecv.at[mine], send_sem=csend.at[0],
+            recv_sem=crcv.at[0], device_id=where, device_id_type=MESH)
 
     @pl.when(owns)
     def _():
         gath[lin] = gpart[mine]
 
-        @pl.loop(1, total)
-        def _(k):
-            src = (lin + k) % total
-            pltpu.make_async_remote_copy(
-                src_ref=gpart.at[0], dst_ref=gath.at[src], send_sem=gsend.at[0],
-                recv_sem=grecv.at[src], device_id=where_is(src), device_id_type=MESH).wait_recv()
-
+        settle(gath.at[pl.ds(0, total - 1)], grecv.at[0])
         packed = jnp.sum(gath[...], axis=0)
         square = jnp.concatenate([packed[:, q * NB : (q + 1) * NB] for q in range(NB // 8)], axis=0)
         flipped = jnp.transpose(square)
@@ -487,44 +497,18 @@
         for away in range(total - 1, 0, -1):
             coef_to(away).start()
 
-    @pl.loop(0, slots)
-    def _(slot):
-        sharing = is_shared(slot)
-        block = per * tm + slot - 2
-        inside = (block >= 0) & (block < NB)
-        alone = inside & (HOP * block >= rows * tm) & (HOP * block + JIT + NFFT <= rows * (tm + 1))
-
-        @pl.loop(0, n)
-        def _(dest):
-            theirs = is_theirs(slot, dest)
-
-            @pl.when(sharing & theirs)
-            def _():
-                exchange(slot, dest).wait_send()
-
-            @pl.when((alone | (sharing & jnp.logical_not(theirs))) & (dest != tm))
-            def _():
-                scatter(slot, dest).wait_send()
-
-    @pl.when(tm > 0)
-    def _():
-        scale_copy(0).wait_send()
-
-    @pl.when(tm < n - 1)
-    def _():
-        scale_copy(1).wait_send()
-
-    for f in range(NF):
-        @pl.when(lin != owner(f))
-        def _(f=f):
-            to_owner(f).wait_send()
-
-    for f in range(NF):
-        @pl.when(lin != owner(f))
-        def _(f=f):
-            pltpu.make_async_remote_copy(
-                src_ref=msg, dst_ref=crecv.at[f], send_sem=csend.at[f], recv_sem=crcv.at[f],
-                device_id=where_is(owner(f)), device_id_type=MESH).wait_recv()
+    for tm_at in range(n):
+        @pl.when(tm == tm_at)
+        def _(tm_at=tm_at):
+            settle(sendp.at[pl.ds(0, half_n * counts[tm_at])], psend.at[0])
+            settle(sendb.at[pl.ds(0, (n - 1) * alone[tm_at] + (half_n - 1) * counts[tm_at])], asend.at[0])
+            groups = sum(half_n // 2 if tm_at + side == half_n else half_n
+                         for side in range(2) if 0 < tm_at + side < n)
+            settle(scales.at[pl.ds(0, groups)], ssend.at[0])
+
+    sent = jnp.where(owns, NF - 1, NF)
+    settle_count(gpart, sent, gsend.at[0], [NF - 1, NF])
+    settle_count(crecv, sent, crcv.at[0], [NF - 1, NF])
 
     lanes = lax.broadcasted_iota(jnp.int32, (NB, 2 * NB), 1)
     signs = jnp.where(lanes < NB, 1.0, -1.0).astype(jnp.bfloat16)
@@ -548,8 +532,7 @@
 
     @pl.when(owns)
     def _():
-        for away in range(total - 1, 0, -1):
-            coef_to(away).wait_send()
+        settle(gath.at[pl.ds(0, total - 1)], csend.at[0])
 
 
 def fused(n, nf_dev, chosen, snapshots, block_starts, freq_index):
@@ -574,11 +557,11 @@
             pltpu.VMEM((NB * 6, 6 * NB), f32),
             pltpu.VMEM((n // 2, 3, rows, 2 * pw), bf16),
             pltpu.VMEM((n, slots * ROWS, 3 * pw), f32),
-            pltpu.VMEM((slots, n, ROWS, 3 * pw), jnp.int16),
-            pltpu.VMEM((slots, n, ROWS, 3 * pw), jnp.int16),
-            pltpu.VMEM((2, slots // 2 * n, 128), f32),
-            pltpu.VMEM((2, slots // 2 * n, 128), f32),
-            pltpu.VMEM((slots, n, ROWS, 3 * pw), bf16),
+            pltpu.VMEM((slots * n, ROWS, 3 * pw), jnp.int16),
+            pltpu.VMEM((slots * n, ROWS, 3 * pw), jnp.int16),
+            pltpu.VMEM((n, slots, 128), f32),
+            pltpu.VMEM((n, slots, 128), f32),
+            pltpu.VMEM((slots * n, ROWS, 3 * pw), bf16),
             pltpu.VMEM((NB, ROWS, 3 * pw), bf16),
             pltpu.VMEM((3, NB * (ROWS + 8), pw), f32),
             pltpu.VMEM((NF, 6 * NB, pw), bf16),
@@ -586,8 +569,8 @@
             pltpu.VMEM((total, NB // 4, 4 * NB), f32),
             pltpu.VMEM((NB // 2, 4 * NB), bf16),
             pltpu.VMEM((NF, NB // 2, 4 * NB), bf16),
-            dma((2 + 3 * n // 2,)), dma((slots, n)), dma((slots, n)), dma((2,)), dma((2,)),
-            dma((slots, n)), dma((NB,)), dma((NF,)), dma((total,)), dma((total,)), dma((NF,)),
+            dma((2 + n // 2,)), dma((1,)), dma((n,)), dma((1,)), dma((n,)),
+            dma((1,)), dma((1,)), dma((1,)), dma((1,)), dma((1,)), dma((1,)),
         ],
         compiler_params=pltpu.CompilerParams(
             collective_id=0, has_side_effects=True, vmem_limit_bytes=54_000_000),

time: 54.5 us -> 47.3 us (0.87)
  Pallas kernels: 51 us -> 43.8 us
    pallas_call x1, Pallas kernels: 51 us -> 43.8 us  [fused(): pl.pallas_call(functools.partial(kernel, n, nf_dev, per, whole, shared, h...]
where the time goes in v3:
time: 47.3 us; the launch traced here: 47.1 us
  Pallas kernels  43.8 us (93%)
  local copies, waits for them, and re-layouts  2.7 us (6%)
  between operations  0.65 us (1%)
    pallas_call x1, Pallas kernels, fused(): pl.pallas_call(functools.partial(kernel, n, nf_dev, per, whole, shared, h...  43.8 us
    unnamed x6, local copies, waits for them, and re-layouts  2.7 us

profile of v3, /device:TPU:0, one launch (start us, length us, event | category | flops | bytes accessed | tf_op | source)
XLA Modules:
  0.0 47.1 jit_solution(6561489229465336641)
XLA Ops:
  0.6 0.0 copy-start
  0.6 0.6 %copy-done = s32[32]{0:T(128)S(1)} copy-done((s32[32]{0:T(128)S(1)}, s32[32]{0:T(128)}, u32[]{:S(2)}) %copy-start) | copy-done | bytes 152
  1.3 0.0 copy-start.1
  1.3 0.7 %copy-done.1 = s32[16]{0:T(128)S(1)} copy-done((s32[16]{0:T(128)S(1)}, s32[16]{0:T(128)}, u32[]{:S(2)}) %copy-start.1) | copy-done | bytes 88
  1.9 43.8 %shard_map.50 = (bf16[3072,128]{1,0:T(8,128)(2,1)S(1)}, f32[1,16]{1,0:T(1,128)S(1)}) custom-call(bf16[3,544,1024]{2,1,0:T(8,128)(2,1)} %bitcast.7, s32[32]{0:T(128)S(1)} %copy-done, s32[16]{0:T(128)S(1)} %copy-done.1), custom_call_target="tpu_custom_call" | custom-call | tf_op jit(solution)/shard_map/pallas_call | solution.py:547
  45.7 0.9 %copy.7 = bf16[16,32,2,3,128]{4,2,3,1,0:T(2,128)(2,1)} copy(bf16[16,32,2,3,128]{4,2,3,1,0:T(2,128)(2,1)S(1)} %bitcast.5) | data formatting | bytes 1572864
  46.6 0.5 %copy.8 = f32[16]{0:T(128)} copy(f32[16]{0:T(128)S(1)} %bitcast.6) | data formatting | bytes 128
Async XLA Ops:
  0.6 0.7 %copy-start = (s32[32]{0:T(128)S(1)}, s32[32]{0:T(128)}, u32[]{:S(2)}) copy-start(s32[32]{0:T(128)} %starts_hbm.1) | copy-start | bytes 388
  1.3 0.7 %copy-start.1 = (s32[16]{0:T(128)S(1)}, s32[16]{0:T(128)}, u32[]{:S(2)}) copy-start(s32[16]{0:T(128)} %freqs_hbm.1) | copy-start | bytes 196

commit v4 on v3

--- a/solution.py
+++ b/solution.py
@@ -161,20 +161,6 @@
     return jnp.dot(base, pick, preferred_element_type=jnp.float32).astype(jnp.bfloat16)
 
 
-def expanders(spread_ref, mask_ref):
-    row = lax.broadcasted_iota(jnp.int32, (NB * 6, 2 * NB), 0)
-    col = lax.broadcasted_iota(jnp.int32, (NB * 6, 2 * NB), 1)
-    first = 6 * (col & (NB - 1))
-    hit = (row >= first) & (row < first + 6) & ((row & 1) == jnp.where(col >= NB, 1, 0))
-    spread_ref[...] = jnp.where(hit, 1.0, 0.0).astype(jnp.bfloat16)
-    row = lax.broadcasted_iota(jnp.int32, (NB * 6, 6 * NB), 0)
-    col = lax.broadcasted_iota(jnp.int32, (NB * 6, 6 * NB), 1)
-    pair = row >> 1
-    comp = pair - 3 * ((pair * 43691) >> 17)
-    part = jnp.where(col >= 4 * NB, 2, jnp.where(col >= 2 * NB, 1, 0))
-    mask_ref[...] = jnp.where(comp == part, 1.0, 0.0)
-
-
 def member(index, devs):
     if not devs:
         return None
@@ -186,8 +172,17 @@
     return hit
 
 
+def division(n, tm, side, dest):
+    edge, half = tm + side, n // 2
+    middle = edge == half
+    left = dest < half
+    all_mine = middle & (left == (tm < half))
+    theirs = (middle & (all_mine ^ True)) | ((middle ^ True) & (dest % 2 != tm % 2))
+    return theirs, middle, all_mine
+
+
 def kernel(n, nf_dev, per, whole, shared, holders, points, x_hbm, starts_hbm, freqs_hbm,
-           modes_ref, energy_ref, starts_ref, freqs_ref, t_ref, spread_ref, mask_ref, xv, parts,
+           modes_ref, energy_ref, starts_ref, freqs_ref, t_ref, stage, xv, parts,
            sendp, others, scales, oscales, sendb, recvb, spec32, spec, gpart, gath, msg, crecv,
            load_sem, psend, precv, ssend, srecv, asend, arecv, gsend, grecv, csend, crcv):
     tm = lax.axis_index("tm")
@@ -210,6 +205,11 @@
     def where_is(index):
         return {"tm": index // nf_dev, "freq": index % nf_dev}
 
+    def displaced(away):
+        row, col = tm + away // nf_dev, fr + away % nf_dev
+        return {"tm": jnp.where(row >= n, row - n, row),
+                "freq": jnp.where(col >= nf_dev, col - nf_dev, col)}
+
     def group(k):
         return jnp.where(tm < half_n, half_n - 1 - k, k)
 
@@ -227,9 +227,8 @@
             load(group(k), c).start()
     barrier = pltpu.get_barrier_semaphore()
 
-    @pl.loop(1, total)
-    def _(k):
-        pl.semaphore_signal(barrier, inc=1, device_id=where_is((lin + k) % total), device_id_type=MESH)
+    for away in range(total - 1, 0, -1):
+        pl.semaphore_signal(barrier, inc=1, device_id=displaced(away), device_id_type=MESH)
 
     small.wait()
     base = base_table(freqs_ref)
@@ -241,7 +240,6 @@
         shift = jnp.where(inside, rows * tm - start, 4 * (rows + NFFT))
         t_ref[slot * ROWS : (slot + 1) * ROWS, :] = shifted(base, shift, rows)
     scales[...] = jnp.zeros_like(scales)
-    expanders(spread_ref, mask_ref)
 
     def low(slot):
         return slot < half_slots
@@ -262,9 +260,7 @@
         return inside & (HOP * block < edge) & (HOP * block + JIT + NFFT > edge)
 
     def is_theirs(slot, dest):
-        middle = tm + pick(low(slot), 0, 1) == half_n
-        by_half = (dest < half_n) != (tm < half_n)
-        return (middle & by_half) | (jnp.logical_not(middle) & (dest % 2 != parity))
+        return division(n, tm, slot // half_slots, dest)[0]
 
     def exchange(slot, dest):
         return pltpu.make_async_remote_copy(
@@ -295,9 +291,6 @@
 
     def edge_exists(side):
         return pick(side == 0, tm > 0, tm < n - 1)
-
-    def at_middle(side):
-        return tm + side == half_n
 
     def sharing(side):
         return sum(jnp.where(is_shared(side * half_slots + k), 1, 0) for k in range(half_slots))
@@ -347,23 +340,42 @@
                         encode(slot, g, d)
 
         for side in range(2):
-            @pl.when(edge_exists(side) & (jnp.logical_not(at_middle(side)) | is_theirs(side * half_slots, 2 * g)))
+            _, whole_group, all_mine = division(n, tm, side, 2 * g)
+
+            @pl.when(edge_exists(side) & jnp.logical_not(whole_group & all_mine))
             def _(side=side):
                 scale_copy(side, g).start()
 
         for d in range(2):
             for slot in range(slots):
                 if shared[slot]:
-                    @pl.when(member(tm, shared[slot]) & is_theirs(slot, 2 * g + d))
+                    @pl.when(member(tm, shared[slot]) & is_theirs(slot, 2 * g + d) & (parity == (0 if slot >= half_slots else 1)))
                     def _(slot=slot, d=d):
                         exchange(slot, 2 * g + d).start()
 
         for d in range(2):
             for slot in range(slots):
                 if whole[slot]:
-                    @pl.when(member(tm, whole[slot]))
+                    @pl.when(member(tm, whole[slot]) & (parity == d))
                     def _(slot=slot, d=d):
                         deliver(slot, 2 * g + d, parts[2 * g + d, slot * ROWS : (slot + 1) * ROWS, :])
+
+        for d in range(2):
+            for slot in range(slots):
+                if shared[slot]:
+                    @pl.when(member(tm, shared[slot]) & is_theirs(slot, 2 * g + d) & (parity == (1 if slot >= half_slots else 0)))
+                    def _(slot=slot, d=d):
+                        exchange(slot, 2 * g + d).start()
+
+    def send_crossing():
+        @pl.loop(0, half_n)
+        def _(k):
+            dest = 2 * group(k) + 1 - parity
+            for slot in range(slots):
+                if whole[slot]:
+                    @pl.when(member(tm, whole[slot]))
+                    def _(slot=slot):
+                        deliver(slot, dest, parts[dest, slot * ROWS : (slot + 1) * ROWS, :])
 
     counts = [sum(tm_at in devs for devs in shared) for tm_at in range(n)]
 
@@ -374,12 +386,12 @@
         @pl.loop(0, half_n)
         def _(k):
             g = group(k)
-            middle = at_middle(side)
-
-            @pl.when(edge_exists(side) & (jnp.logical_not(middle) | jnp.logical_not(is_theirs(side * half_slots, 2 * g))))
+            _, whole_group, all_mine = division(n, tm, side, 2 * g)
+
+            @pl.when(edge_exists(side) & (jnp.logical_not(whole_group) | all_mine))
             def _():
                 settle(oscales.at[side * half_n + g], srecv.at[side * half_n + g])
-                settle_count(others, sharing(side) * jnp.where(middle, 2, 1), precv.at[side * half_n + g],
+                settle_count(others, sharing(side) * jnp.where(whole_group, 2, 1), precv.at[side * half_n + g],
                              [count * twice for count in range(1, half_slots + 1) for twice in (1, 2)])
                 for d in range(2):
                     dest = 2 * g + d
@@ -395,6 +407,10 @@
                             deliver(slot, dest, here + other * (peak * (1.0 / 32767.0)))
 
 
+            @pl.when((turn == 0) & (k == half_n - 1))
+            def _():
+                send_crossing()
+
     alone = [sum(tm_at in devs for devs in whole) for tm_at in range(n)]
     for tm_at in range(n):
         @pl.when(tm == tm_at)
@@ -414,13 +430,13 @@
 
     upper = lax.broadcasted_iota(jnp.int32, (NB, NB), 1) >= lax.broadcasted_iota(jnp.int32, (NB, NB), 0)
     for f in range(NF):
-        real = [spec32[c, pl.ds(2 * f, NB, stride=pitch), :].astype(jnp.bfloat16) for c in range(3)]
-        imag = [spec32[c, pl.ds(2 * f + 1, NB, stride=pitch), :].astype(jnp.bfloat16) for c in range(3)]
-        for c in range(3):
-            spec[f, c * 2 * NB : c * 2 * NB + NB, :] = real[c]
-            spec[f, c * 2 * NB + NB : (c + 1) * 2 * NB, :] = imag[c]
-        lhs = jnp.concatenate(real + imag, axis=1)
-        rhs = jnp.concatenate([lhs, jnp.concatenate(imag + [-v for v in real], axis=1)], axis=0)
+        real, imag = [jnp.concatenate([
+            spec32[c, pl.ds(2 * f + r, NB, stride=pitch), :].astype(jnp.bfloat16)
+            for c in range(3)], axis=1) for r in range(2)]
+        spec[f, :NB, :] = real
+        spec[f, NB:, :] = imag
+        lhs = jnp.concatenate([real, imag], axis=1)
+        rhs = jnp.concatenate([lhs, jnp.concatenate([imag, -real], axis=1)], axis=0)
         gram = lax.dot_general(lhs, rhs, (((1,), (1,)), ((), ())), preferred_element_type=jnp.float32)
         packed = jnp.where(upper, gram[:, :NB], gram[:, NB:])
         gpart[f] = jnp.concatenate([packed[8 * q : 8 * q + 8] for q in range(NB // 8)], axis=1)
@@ -431,12 +447,9 @@
                     to_owner(sent).start()
 
     def coef_to(away):
-        row, col = tm + away // nf_dev, fr + away % nf_dev
-        where = {"tm": jnp.where(row >= n, row - n, row),
-                 "freq": jnp.where(col >= nf_dev, col - nf_dev, col)}
         return pltpu.make_async_remote_copy(
             src_ref=msg, dst_ref=crecv.at[mine], send_sem=csend.at[0],
-            recv_sem=crcv.at[0], device_id=where, device_id_type=MESH)
+            recv_sem=crcv.at[0], device_id=displaced(away), device_id_type=MESH)
 
     @pl.when(owns)
     def _():
@@ -498,12 +511,21 @@
             coef_to(away).start()
 
     for tm_at in range(n):
+        handed, groups = 0, 0
+        for slot in range(slots):
+            if tm_at in shared[slot]:
+                handed += sum(division(n, tm_at, slot // half_slots, dest)[0] for dest in range(n))
+        for side in range(2):
+            if 0 < tm_at + side < n:
+                for g in range(half_n):
+                    _, whole_group, all_mine = division(n, tm_at, side, 2 * g)
+                    groups += not (whole_group and all_mine)
+
         @pl.when(tm == tm_at)
-        def _(tm_at=tm_at):
-            settle(sendp.at[pl.ds(0, half_n * counts[tm_at])], psend.at[0])
-            settle(sendb.at[pl.ds(0, (n - 1) * alone[tm_at] + (half_n - 1) * counts[tm_at])], asend.at[0])
-            groups = sum(half_n // 2 if tm_at + side == half_n else half_n
-                         for side in range(2) if 0 < tm_at + side < n)
+        def _(tm_at=tm_at, handed=handed, groups=groups):
+            settle(sendp.at[pl.ds(0, handed)], psend.at[0])
+            own = n * (alone[tm_at] + counts[tm_at]) - handed
+            settle(sendb.at[pl.ds(0, own - alone[tm_at] - counts[tm_at])], asend.at[0])
             settle(scales.at[pl.ds(0, groups)], ssend.at[0])
 
     sent = jnp.where(owns, NF - 1, NF)
@@ -523,11 +545,11 @@
         straight = jnp.where(hidden, jnp.zeros_like(straight), straight)
         crossed = jnp.concatenate([straight[:, NB:], straight[:, :NB]], axis=1)
         stacked = jnp.concatenate([straight * signs, crossed], axis=0)
-        tiled = jnp.concatenate([stacked] * 3, axis=1)
-        full = jnp.dot(spread_ref[...], tiled, preferred_element_type=jnp.float32)
-        full = (full * mask_ref[...]).astype(jnp.bfloat16)
-        modes_ref[f * 6 * NB : (f + 1) * 6 * NB, :] = jnp.dot(
-            full, spec[f], preferred_element_type=jnp.float32).astype(jnp.bfloat16)
+        out = jnp.dot(stacked, spec[f], preferred_element_type=jnp.float32)
+        for c in range(3):
+            for o in range(2):
+                stage[f % 4, pl.ds(2 * c + o, NB, stride=6), :] = out[o * NB : (o + 1) * NB, c * pw : (c + 1) * pw]
+        modes_ref[f * 6 * NB : (f + 1) * 6 * NB, :] = stage[f % 4].astype(jnp.bfloat16)
     energy_ref[...] = energies
 
     @pl.when(owns)
@@ -553,8 +575,7 @@
             pltpu.SMEM((NB,), jnp.int32),
             pltpu.SMEM((NF,), jnp.int32),
             pltpu.VMEM((slots * ROWS, rows), bf16),
-            pltpu.VMEM((NB * 6, 2 * NB), bf16),
-            pltpu.VMEM((NB * 6, 6 * NB), f32),
+            pltpu.VMEM((4, 6 * NB, pw), f32),
             pltpu.VMEM((n // 2, 3, rows, 2 * pw), bf16),
             pltpu.VMEM((n, slots * ROWS, 3 * pw), f32),
             pltpu.VMEM((slots * n, ROWS, 3 * pw), jnp.int16),
@@ -564,7 +585,7 @@
             pltpu.VMEM((slots * n, ROWS, 3 * pw), bf16),
             pltpu.VMEM((NB, ROWS, 3 * pw), bf16),
             pltpu.VMEM((3, NB * (ROWS + 8), pw), f32),
-            pltpu.VMEM((NF, 6 * NB, pw), bf16),
+            pltpu.VMEM((NF, 2 * NB, 3 * pw), bf16),
             pltpu.VMEM((NF, NB // 4, 4 * NB), f32),
             pltpu.VMEM((total, NB // 4, 4 * NB), f32),
             pltpu.VMEM((NB // 2, 4 * NB), bf16),

time: 47.3 us -> 45.3 us (0.958)
  Pallas kernels: 43.8 us -> 41.8 us
    pallas_call x1, Pallas kernels: 43.8 us -> 41.8 us  [fused(): pl.pallas_call(functools.partial(kernel, n, nf_dev, per, whole, shared, h...]
where the time goes in v4:
time: 45.3 us; the launch traced here: 45.1 us
  Pallas kernels  41.8 us (92%)
  local copies, waits for them, and re-layouts  2.7 us (6%)
  between operations  0.65 us (1%)
    pallas_call x1, Pallas kernels, fused(): pl.pallas_call(functools.partial(kernel, n, nf_dev, per, whole, shared, h...  41.8 us
    unnamed x6, local copies, waits for them, and re-layouts  2.7 us

profile of v4, /device:TPU:0, one launch (start us, length us, event | category | flops | bytes accessed | tf_op | source)
XLA Modules:
  0.0 45.1 jit_solution(13619883097756254026)
XLA Ops:
  0.6 0.0 copy-start
  0.6 0.6 %copy-done = s32[32]{0:T(128)S(1)} copy-done((s32[32]{0:T(128)S(1)}, s32[32]{0:T(128)}, u32[]{:S(2)}) %copy-start) | copy-done | bytes 152
  1.3 0.0 copy-start.1
  1.3 0.7 %copy-done.1 = s32[16]{0:T(128)S(1)} copy-done((s32[16]{0:T(128)S(1)}, s32[16]{0:T(128)}, u32[]{:S(2)}) %copy-start.1) | copy-done | bytes 88
  1.9 41.8 %shard_map.50 = (bf16[3072,128]{1,0:T(8,128)(2,1)S(1)}, f32[1,16]{1,0:T(1,128)S(1)}) custom-call(bf16[3,544,1024]{2,1,0:T(8,128)(2,1)} %bitcast.7, s32[32]{0:T(128)S(1)} %copy-done, s32[16]{0:T(128)S(1)} %copy-done.1), custom_call_target="tpu_custom_call" | custom-call | tf_op jit(solution)/shard_map/pallas_call | solution.py:569
  43.7 0.9 %copy.7 = bf16[16,32,2,3,128]{4,2,3,1,0:T(2,128)(2,1)} copy(bf16[16,32,2,3,128]{4,2,3,1,0:T(2,128)(2,1)S(1)} %bitcast.5) | data formatting | bytes 1572864
  44.6 0.5 %copy.8 = f32[16]{0:T(128)} copy(f32[16]{0:T(128)S(1)} %bitcast.6) | data formatting | bytes 128
Async XLA Ops:
  0.6 0.7 %copy-start = (s32[32]{0:T(128)S(1)}, s32[32]{0:T(128)}, u32[]{:S(2)}) copy-start(s32[32]{0:T(128)} %starts_hbm.1) | copy-start | bytes 388
  1.3 0.7 %copy-start.1 = (s32[16]{0:T(128)S(1)}, s32[16]{0:T(128)}, u32[]{:S(2)}) copy-start(s32[16]{0:T(128)} %freqs_hbm.1) | copy-start | bytes 196

commit v5 on v4

--- a/solution.py
+++ b/solution.py
@@ -138,12 +138,12 @@
     return per, whole, shared, holders
 
 
-def base_table(freqs_ref):
+def base_table(ints_ref):
     row = lax.broadcasted_iota(jnp.int32, (ROWS, NFFT), 0)
     times_idx = lax.broadcasted_iota(jnp.int32, (ROWS, NFFT), 1)
     freqs = jnp.zeros((ROWS, NFFT), jnp.int32)
     for f in range(NF):
-        freqs = jnp.where((row >> 1) == f, freqs_ref[f], freqs)
+        freqs = jnp.where((row >> 1) == f, ints_ref[NB + f], freqs)
     phase = (freqs * times_idx) & (NFFT - 1)
     angles = 2.0 * math.pi / NFFT * phase.astype(jnp.float32)
     window = 0.5 - 0.5 * jnp.cos(2.0 * math.pi / NFFT * times_idx.astype(jnp.float32))
@@ -181,9 +181,9 @@
     return theirs, middle, all_mine
 
 
-def kernel(n, nf_dev, per, whole, shared, holders, points, x_hbm, starts_hbm, freqs_hbm,
-           modes_ref, energy_ref, starts_ref, freqs_ref, t_ref, stage, xv, parts,
-           sendp, others, scales, oscales, sendb, recvb, spec32, spec, gpart, gath, msg, crecv,
+def kernel(n, nf_dev, per, whole, shared, holders, points, x_hbm, ints_hbm,
+           spec, coefs_ref, ints_ref, t_ref, xv, parts,
+           sendp, others, scales, oscales, sendb, recvb, spec32, gpart, gath, msg, crecv,
            load_sem, psend, precv, ssend, srecv, asend, arecv, gsend, grecv, csend, crcv):
     tm = lax.axis_index("tm")
     fr = lax.axis_index("freq")
@@ -216,12 +216,10 @@
     def load(g, c):
         return pltpu.make_async_copy(
             x_hbm.at[c, :, pl.ds(pl.multiple_of(g * 2 * pw, 2 * pw), 2 * pw)], xv.at[g, c],
-            load_sem.at[2 + g])
-
-    small = pltpu.make_async_copy(freqs_hbm, freqs_ref, load_sem.at[0])
+            load_sem.at[1 + g])
+
+    small = pltpu.make_async_copy(ints_hbm, ints_ref, load_sem.at[0])
     small.start()
-    starts = pltpu.make_async_copy(starts_hbm, starts_ref, load_sem.at[1])
-    starts.start()
     for k in range(half_n):
         for c in range(3):
             load(group(k), c).start()
@@ -231,11 +229,10 @@
         pl.semaphore_signal(barrier, inc=1, device_id=displaced(away), device_id_type=MESH)
 
     small.wait()
-    base = base_table(freqs_ref)
-    starts.wait()
+    base = base_table(ints_ref)
     for slot in range(slots):
         block = per * tm + slot - 2
-        start = starts_ref[jnp.clip(block, 0, NB - 1)]
+        start = ints_ref[jnp.clip(block, 0, NB - 1)]
         inside = (block >= 0) & (block < NB)
         shift = jnp.where(inside, rows * tm - start, 4 * (rows + NFFT))
         t_ref[slot * ROWS : (slot + 1) * ROWS, :] = shifted(base, shift, rows)
@@ -322,7 +319,7 @@
     @pl.loop(0, half_n)
     def _(k):
         g = group(k)
-        settle(xv.at[g], load_sem.at[2 + g])
+        settle(xv.at[g], load_sem.at[1 + g])
         for c in range(3):
             part = jnp.dot(t_ref[...], xv[g, c], preferred_element_type=jnp.float32)
             for d in range(2):
@@ -531,6 +528,15 @@
     sent = jnp.where(owns, NF - 1, NF)
     settle_count(gpart, sent, gsend.at[0], [NF - 1, NF])
     settle_count(crecv, sent, crcv.at[0], [NF - 1, NF])
+    coefs_ref[...] = crecv[...]
+
+    @pl.when(owns)
+    def _():
+        settle(gath.at[pl.ds(0, total - 1)], csend.at[0])
+
+
+def finish_kernel(spec, crecv, modes_hbm, energy_hbm, stage, modes_ref, energy_ref, sem):
+    pw = modes_ref.shape[1]
 
     lanes = lax.broadcasted_iota(jnp.int32, (NB, 2 * NB), 1)
     signs = jnp.where(lanes < NB, 1.0, -1.0).astype(jnp.bfloat16)
@@ -550,11 +556,13 @@
             for o in range(2):
                 stage[f % 4, pl.ds(2 * c + o, NB, stride=6), :] = out[o * NB : (o + 1) * NB, c * pw : (c + 1) * pw]
         modes_ref[f * 6 * NB : (f + 1) * 6 * NB, :] = stage[f % 4].astype(jnp.bfloat16)
+        part = pl.ds(f * 6 * NB, 6 * NB)
+        pltpu.make_async_copy(modes_ref.at[part], modes_hbm.at[part], sem.at[0]).start()
     energy_ref[...] = energies
-
-    @pl.when(owns)
-    def _():
-        settle(gath.at[pl.ds(0, total - 1)], csend.at[0])
+    last = pltpu.make_async_copy(energy_ref, energy_hbm, sem.at[1])
+    last.start()
+    pltpu.make_async_copy(modes_ref, modes_hbm, sem.at[0]).wait()
+    last.wait()
 
 
 def fused(n, nf_dev, chosen, snapshots, block_starts, freq_index):
@@ -566,16 +574,15 @@
     f32, bf16 = jnp.float32, jnp.bfloat16
     dma = pltpu.SemaphoreType.DMA
     vmem = pl.BlockSpec(memory_space=pltpu.VMEM)
-    modes, energy = pl.pallas_call(
+    spec, coefs = pl.pallas_call(
         functools.partial(kernel, n, nf_dev, per, whole, shared, holders, float(wide * nf_dev)),
-        out_shape=(jax.ShapeDtypeStruct((NF * NB * 6, pw), bf16), jax.ShapeDtypeStruct((1, NF), f32)),
-        in_specs=[pl.BlockSpec(memory_space=pltpu.HBM)] * 3,
+        out_shape=(jax.ShapeDtypeStruct((NF, 2 * NB, 3 * pw), bf16),
+                   jax.ShapeDtypeStruct((NF, NB // 2, 4 * NB), bf16)),
+        in_specs=[pl.BlockSpec(memory_space=pltpu.HBM)] * 2,
         out_specs=(vmem, vmem),
         scratch_shapes=[
-            pltpu.SMEM((NB,), jnp.int32),
-            pltpu.SMEM((NF,), jnp.int32),
+            pltpu.SMEM((NB + NF,), jnp.int32),
             pltpu.VMEM((slots * ROWS, rows), bf16),
-            pltpu.VMEM((4, 6 * NB, pw), f32),
             pltpu.VMEM((n // 2, 3, rows, 2 * pw), bf16),
             pltpu.VMEM((n, slots * ROWS, 3 * pw), f32),
             pltpu.VMEM((slots * n, ROWS, 3 * pw), jnp.int16),
@@ -585,17 +592,27 @@
             pltpu.VMEM((slots * n, ROWS, 3 * pw), bf16),
             pltpu.VMEM((NB, ROWS, 3 * pw), bf16),
             pltpu.VMEM((3, NB * (ROWS + 8), pw), f32),
-            pltpu.VMEM((NF, 2 * NB, 3 * pw), bf16),
             pltpu.VMEM((NF, NB // 4, 4 * NB), f32),
             pltpu.VMEM((total, NB // 4, 4 * NB), f32),
             pltpu.VMEM((NB // 2, 4 * NB), bf16),
             pltpu.VMEM((NF, NB // 2, 4 * NB), bf16),
-            dma((2 + n // 2,)), dma((1,)), dma((n,)), dma((1,)), dma((n,)),
+            dma((1 + n // 2,)), dma((1,)), dma((n,)), dma((1,)), dma((n,)),
             dma((1,)), dma((1,)), dma((1,)), dma((1,)), dma((1,)), dma((1,)),
         ],
         compiler_params=pltpu.CompilerParams(
             collective_id=0, has_side_effects=True, vmem_limit_bytes=54_000_000),
-    )(jnp.transpose(snapshots, (1, 0, 2)), block_starts, freq_index)
+    )(jnp.transpose(snapshots, (1, 0, 2)), jnp.concatenate([block_starts, freq_index]))
+    modes, energy = pl.pallas_call(
+        finish_kernel,
+        out_shape=(jax.ShapeDtypeStruct((NF * NB * 6, pw), bf16), jax.ShapeDtypeStruct((1, NF), f32)),
+        in_specs=[vmem, vmem],
+        out_specs=[pl.BlockSpec(memory_space=pltpu.HBM)] * 2,
+        scratch_shapes=[
+            pltpu.VMEM((4, 6 * NB, pw), f32), pltpu.VMEM((NF * NB * 6, pw), bf16),
+            pltpu.VMEM((1, NF), f32), dma((2,)),
+        ],
+        compiler_params=pltpu.CompilerParams(vmem_limit_bytes=8_000_000),
+    )(spec, coefs)
     modes = modes.reshape(NF, NB, 3, 2, pw).transpose(0, 1, 3, 2, 4)
     return modes, energy.reshape(NF)
 

time: 45.3 us -> 44 us (0.971)
  local copies, waits for them, and re-layouts: 2.7 us -> 0 us
  other arithmetic: 0 us -> 0.75 us
  Pallas kernels: 41.8 us -> 42.5 us
    unnamed x6 -> x0, local copies, waits for them, and re-layouts: 2.7 us -> none
    pallas_call x0 -> x1, Pallas kernels: none -> 1.29 us  [fused(): pl.pallas_call(finish_kernel, out_shape=(jax.ShapeDtypeStruct((NF * NB *...]
    concatenate x0 -> x1, other arithmetic: none -> 0.75 us  [fused(): jnp.concatenate([block_starts, freq_index])]
    pallas_call x1, Pallas kernels: 41.8 us -> 41.2 us  [fused(): pl.pallas_call(functools.partial(kernel, n, nf_dev, per, whole, shared, h...]
where the time goes in v5:
time: 44 us; the launch traced here: 43.8 us
  Pallas kernels  42.5 us (97%)
  other arithmetic  0.75 us (2%)
  between operations  0.64 us (1%)
    pallas_call x1, Pallas kernels, fused(): pl.pallas_call(functools.partial(kernel, n, nf_dev, per, whole, shared, h...  41.2 us
    pallas_call x1, Pallas kernels, fused(): pl.pallas_call(finish_kernel, out_shape=(jax.ShapeDtypeStruct((NF * NB *...  1.29 us

profile of v5, /device:TPU:0, one launch (start us, length us, event | category | flops | bytes accessed | tf_op | source)
XLA Modules:
  0.0 43.8 jit_solution(2479461777180636748)
XLA Ops:
  0.6 0.7 %pad_add_fusion.ints_hbm = s32[48]{0:T(128)S(1)} fusion(s32[16]{0:T(128)} %param.5, s32[32]{0:T(128)} %param.4), kind=kLoop, calls=%fused_computation | loop fusion | flops 48 | bytes 384 | tf_op jit(solution)/shard_map/concatenate | solution.py:604
  1.4 41.2 %shard_map.50 = (bf16[16,64,384]{2,1,0:T(8,128)(2,1)S(1)}, bf16[16,16,128]{2,1,0:T(8,128)(2,1)S(1)}) custom-call(bf16[3,544,1024]{2,1,0:T(8,128)(2,1)} %bitcast.5, s32[48]{0:T(128)S(1)} %pad_add_fusion.ints_hbm), custom_call_target="tpu_custom_call" | custom-call | tf_op jit(solution)/shard_map/pallas_call | solution.py:577
  42.6 1.3 %shard_map.51 = (bf16[3072,128]{1,0:T(8,128)(2,1)}, f32[1,16]{1,0:T(1,128)}) custom-call(bf16[16,64,384]{2,1,0:T(8,128)(2,1)S(1)} %get-tuple-element.6.spec, bf16[16,16,128]{2,1,0:T(8,128)(2,1)S(1)} %get-tuple-element.7.crecv), custom_call_target="tpu_custom_call" | custom-call | tf_op jit(solution)/shard_map/pallas_call | solution.py:605

commit v6 on v5

--- a/solution.py
+++ b/solution.py
@@ -108,7 +108,7 @@
 
 
 def plan(n, rows, total, width):
-    if n < 2 or n % 2 or NB % n or total % (2 * NF) or width != 128 or rows % 16:
+    if n % 4 or NB % n or total % (2 * NF) or width != 128 or rows % 16:
         return None
     per = NB // n
     if per < 4 or per % 2:
@@ -183,8 +183,8 @@
 
 def kernel(n, nf_dev, per, whole, shared, holders, points, x_hbm, ints_hbm,
            spec, coefs_ref, ints_ref, t_ref, xv, parts,
-           sendp, others, scales, oscales, sendb, recvb, spec32, gpart, gath, msg, crecv,
-           load_sem, psend, precv, ssend, srecv, asend, arecv, gsend, grecv, csend, crcv):
+           sendp, others, relayb, scales, oscales, sendb, recvb, spec32, gpart, gath, msg, crecv,
+           load_sem, psend, precv, rrecv, fsend, ssend, srecv, asend, arecv, gsend, grecv, csend, crcv):
     tm = lax.axis_index("tm")
     fr = lax.axis_index("freq")
     total = n * nf_dev
@@ -259,9 +259,10 @@
     def is_theirs(slot, dest):
         return division(n, tm, slot // half_slots, dest)[0]
 
-    def exchange(slot, dest):
+    def exchange(slot, length, dest):
         return pltpu.make_async_remote_copy(
-            src_ref=sendp.at[slot * n + dest], dst_ref=others.at[across(slot) * n + dest],
+            src_ref=sendp.at[pl.ds(dest * slots + slot, length)],
+            dst_ref=others.at[pl.ds(dest * slots + across(slot), length)],
             send_sem=psend.at[0], recv_sem=precv.at[across(slot) // half_slots * half_n + dest // 2],
             device_id={"tm": partner(slot), "freq": fr}, device_id_type=MESH)
 
@@ -271,9 +272,10 @@
             send_sem=ssend.at[0], recv_sem=srecv.at[(1 - side) * half_n + g],
             device_id={"tm": partner(side * half_slots), "freq": fr}, device_id_type=MESH)
 
-    def scatter(slot, dest):
+    def scatter(slot, length, dest):
+        block = per * tm + slot - 2
         return pltpu.make_async_remote_copy(
-            src_ref=sendb.at[slot * n + dest], dst_ref=recvb.at[per * tm + slot - 2],
+            src_ref=sendb.at[pl.ds(dest * slots + slot, length)], dst_ref=recvb.at[pl.ds(block, length)],
             send_sem=asend.at[0], recv_sem=arecv.at[0],
             device_id={"tm": dest, "freq": fr}, device_id_type=MESH)
 
@@ -292,7 +294,7 @@
     def sharing(side):
         return sum(jnp.where(is_shared(side * half_slots + k), 1, 0) for k in range(half_slots))
 
-    def deliver(slot, dest, value):
+    def put(slot, dest, value):
         value = value.astype(jnp.bfloat16)
 
         @pl.when(dest == tm)
@@ -301,8 +303,83 @@
 
         @pl.when(dest != tm)
         def _():
-            sendb[slot * n + dest] = value
-            scatter(slot, dest).start()
+            sendb[dest * slots + slot] = value
+
+    def first_shared(side):
+        flags = [is_shared(side * half_slots + k) for k in range(half_slots)]
+        first = half_slots - 1
+        for k in range(half_slots - 2, -1, -1):
+            first = jnp.where(flags[k], k, first)
+        return side * half_slots + first
+
+    def runs(table):
+        found = {}
+        for tm_at in range(n):
+            slot = 0
+            while slot < slots:
+                length = 0
+                while slot + length < slots and tm_at in table[slot + length]:
+                    length += 1
+                if length:
+                    found.setdefault((slot, length), []).append(tm_at)
+                slot += length + 1
+        return found
+
+    def hops(dest):
+        return ((tm == 1) & (dest >= half_n)) | ((tm == n - 2) & (dest < half_n))
+
+    def relay_rank(dest):
+        return dest // 2 % (half_n // 2)
+
+    def to_relay(first, length, place, dest):
+        return pltpu.make_async_remote_copy(
+            src_ref=sendb.at[pl.ds(dest * slots + first, length)], dst_ref=relayb.at[pl.ds(place, length)],
+            send_sem=asend.at[0], recv_sem=rrecv.at[0],
+            device_id={"tm": tm + 1 - 2 * parity, "freq": fr}, device_id_type=MESH)
+
+    def relay_runs(source):
+        placed, place = [], 0
+        for (first, length), devs in runs(whole).items():
+            if source in devs:
+                placed.append((first, length, place))
+                place += length * (half_n // 2)
+        return placed, place
+
+    def send_to_relay(dest):
+        for source in (1, n - 2):
+            @pl.when((tm == source) & hops(dest))
+            def _(source=source):
+                for first, length, place in relay_runs(source)[0]:
+                    for slot in range(first, first + length):
+                        sendb[dest * slots + slot] = parts[dest, slot * ROWS : (slot + 1) * ROWS, :].astype(jnp.bfloat16)
+                    to_relay(first, length, place + length * relay_rank(dest), dest).start()
+
+    def relay():
+        for me, source in ((0, 1), (n - 1, n - 2)):
+            @pl.when(tm == me)
+            def _(source=source):
+                placed, amount = relay_runs(source)
+                settle(relayb.at[pl.ds(0, amount)], rrecv.at[0])
+                for first, length, place in placed:
+                    for rank in range(half_n // 2):
+                        dest = 2 * rank + (half_n if source == 1 else 0) + 1 - source % 2
+                        spot = place + length * rank
+                        pltpu.make_async_remote_copy(
+                            src_ref=relayb.at[pl.ds(spot, length)],
+                            dst_ref=recvb.at[pl.ds(per * source + first - 2, length)],
+                            send_sem=fsend.at[0], recv_sem=arecv.at[0],
+                            device_id={"tm": dest, "freq": fr}, device_id_type=MESH).start()
+
+    def send_whole(dest, chosen):
+        for (first, length), devs in runs(whole).items():
+            @pl.when(member(tm, devs) & chosen)
+            def _(first=first, length=length):
+                for slot in range(first, first + length):
+                    put(slot, dest, parts[dest, slot * ROWS : (slot + 1) * ROWS, :])
+
+                @pl.when(dest != tm)
+                def _():
+                    scatter(first, length, dest).start()
 
     diagonal = (lax.broadcasted_iota(jnp.int32, (ROWS, 128), 0)
                 == lax.broadcasted_iota(jnp.int32, (ROWS, 128), 1))
@@ -311,10 +388,13 @@
         value = parts[2 * g + d, slot * ROWS : (slot + 1) * ROWS, :]
         peak = jnp.maximum(jnp.max(jnp.abs(value), axis=1, keepdims=True), 1e-30)
         whole_numbers = (value * (32767.0 / peak) + 12582912.0) - 12582912.0
-        sendp[slot * n + 2 * g + d] = whole_numbers.astype(jnp.int32).astype(jnp.int16)
+        sendp[(2 * g + d) * slots + slot] = whole_numbers.astype(jnp.int32).astype(jnp.int16)
         line = jnp.sum(jnp.where(diagonal, peak, 0.0), axis=0, keepdims=True)
         row = 2 * (slot % half_slots) + d
         scales[slot // half_slots * half_n + g, row : row + 1, :] = line
+
+    lengths = sorted({sum(tm_at in devs for devs in shared[side * half_slots : (side + 1) * half_slots])
+                      for tm_at in range(n) for side in range(2)} - {0})
 
     @pl.loop(0, half_n)
     def _(k):
@@ -343,36 +423,26 @@
             def _(side=side):
                 scale_copy(side, g).start()
 
+        def send_codes(want):
+            for side in range(2):
+                for d in range(2):
+                    theirs = division(n, tm, side, 2 * g + d)[0]
+                    for length in lengths:
+                        @pl.when(edge_exists(side) & theirs & (parity == (want ^ side)) & (sharing(side) == length))
+                        def _(side=side, d=d, length=length):
+                            exchange(first_shared(side), length, 2 * g + d).start()
+
+        send_codes(1)
+        send_to_relay(2 * g + 1 - parity)
         for d in range(2):
-            for slot in range(slots):
-                if shared[slot]:
-                    @pl.when(member(tm, shared[slot]) & is_theirs(slot, 2 * g + d) & (parity == (0 if slot >= half_slots else 1)))
-                    def _(slot=slot, d=d):
-                        exchange(slot, 2 * g + d).start()
-
-        for d in range(2):
-            for slot in range(slots):
-                if whole[slot]:
-                    @pl.when(member(tm, whole[slot]) & (parity == d))
-                    def _(slot=slot, d=d):
-                        deliver(slot, 2 * g + d, parts[2 * g + d, slot * ROWS : (slot + 1) * ROWS, :])
-
-        for d in range(2):
-            for slot in range(slots):
-                if shared[slot]:
-                    @pl.when(member(tm, shared[slot]) & is_theirs(slot, 2 * g + d) & (parity == (1 if slot >= half_slots else 0)))
-                    def _(slot=slot, d=d):
-                        exchange(slot, 2 * g + d).start()
+            send_whole(2 * g + d, parity == d)
+        send_codes(0)
 
     def send_crossing():
         @pl.loop(0, half_n)
         def _(k):
             dest = 2 * group(k) + 1 - parity
-            for slot in range(slots):
-                if whole[slot]:
-                    @pl.when(member(tm, whole[slot]))
-                    def _(slot=slot):
-                        deliver(slot, dest, parts[dest, slot * ROWS : (slot + 1) * ROWS, :])
+            send_whole(dest, jnp.logical_not(hops(dest)))
 
     counts = [sum(tm_at in devs for devs in shared) for tm_at in range(n)]
 
@@ -399,49 +469,64 @@
                         def _(slot=slot, dest=dest, row=2 * index + d):
                             line = oscales[side * half_n + g, row : row + 1, :]
                             peak = jnp.sum(jnp.where(diagonal, line, 0.0), axis=1, keepdims=True)
-                            other = others[slot * n + dest].astype(jnp.int32).astype(jnp.float32)
+                            other = others[dest * slots + slot].astype(jnp.int32).astype(jnp.float32)
                             here = parts[dest, pl.ds(pl.multiple_of(slot * ROWS, ROWS), ROWS), :]
-                            deliver(slot, dest, here + other * (peak * (1.0 / 32767.0)))
-
-
-            @pl.when((turn == 0) & (k == half_n - 1))
+                            put(slot, dest, here + other * (peak * (1.0 / 32767.0)))
+
+                    mine_here = jnp.logical_not(division(n, tm, side, dest)[0]) & (dest != tm)
+                    for length in lengths:
+                        @pl.when(mine_here & (sharing(side) == length))
+                        def _(length=length, dest=dest):
+                            scatter(first_shared(side), length, dest).start()
+
+
+            @pl.when((turn == 0) & (k == 0))
+            def _():
+                relay()
+
+            @pl.when((turn == 0) & (k == 0))
             def _():
                 send_crossing()
 
     alone = [sum(tm_at in devs for devs in whole) for tm_at in range(n)]
-    for tm_at in range(n):
-        @pl.when(tm == tm_at)
-        def _(tm_at=tm_at):
-            settle(recvb.at[pl.ds(0, NB - alone[tm_at] - counts[tm_at])], arecv.at[0])
-
     pitch = spec32.shape[1] // NB
+    missing = [NB - alone[tm_at] - counts[tm_at] for tm_at in range(n)]
+    settle_count(recvb, sum(jnp.where(tm == tm_at, missing[tm_at], 0) for tm_at in range(n)), arecv.at[0], missing)
     for block in range(NB):
         values = recvb[block]
         for c in range(3):
             spec32[c, block * pitch : block * pitch + ROWS, :] = values[:, c * 128 : (c + 1) * 128].astype(jnp.float32)
-
-    def to_owner(f):
-        return pltpu.make_async_remote_copy(
+    for f in range(NF):
+        for r in range(2):
+            spec[f, r * NB : (r + 1) * NB, :] = jnp.concatenate([
+                spec32[c, pl.ds(2 * f + r, NB, stride=pitch), :].astype(jnp.bfloat16)
+                for c in range(3)], axis=1)
+
+    def to_owner(k):
+        first, last = owner(NF - 1 - k), owner(k)
+        near_start = tm < half_n
+        f = jnp.where(near_start, NF - 1 - k, k)
+        place = {"tm": jnp.where(near_start, first // nf_dev, last // nf_dev),
+                 "freq": jnp.where(near_start, first % nf_dev, last % nf_dev)}
+        return f, pltpu.make_async_remote_copy(
             src_ref=gpart.at[f], dst_ref=gath.at[lin], send_sem=gsend.at[0],
-            recv_sem=grecv.at[0], device_id=where_is(owner(f)), device_id_type=MESH)
+            recv_sem=grecv.at[0], device_id=place, device_id_type=MESH)
 
     upper = lax.broadcasted_iota(jnp.int32, (NB, NB), 1) >= lax.broadcasted_iota(jnp.int32, (NB, NB), 0)
     for f in range(NF):
-        real, imag = [jnp.concatenate([
-            spec32[c, pl.ds(2 * f + r, NB, stride=pitch), :].astype(jnp.bfloat16)
-            for c in range(3)], axis=1) for r in range(2)]
-        spec[f, :NB, :] = real
-        spec[f, NB:, :] = imag
+        real, imag = spec[f, :NB, :], spec[f, NB:, :]
         lhs = jnp.concatenate([real, imag], axis=1)
         rhs = jnp.concatenate([lhs, jnp.concatenate([imag, -real], axis=1)], axis=0)
         gram = lax.dot_general(lhs, rhs, (((1,), (1,)), ((), ())), preferred_element_type=jnp.float32)
         packed = jnp.where(upper, gram[:, :NB], gram[:, NB:])
         gpart[f] = jnp.concatenate([packed[8 * q : 8 * q + 8] for q in range(NB // 8)], axis=1)
-        if f % 4 == 3:
-            for sent in range(f - 3, f + 1):
-                @pl.when(lin != owner(sent))
-                def _(sent=sent):
-                    to_owner(sent).start()
+        if f % 16 == 15:
+            for sent in range(f - 15, f + 1):
+                target, copy = to_owner(sent)
+
+                @pl.when(lin != owner(target))
+                def _(copy=copy):
+                    copy.start()
 
     def coef_to(away):
         return pltpu.make_async_remote_copy(
@@ -524,6 +609,8 @@
             own = n * (alone[tm_at] + counts[tm_at]) - handed
             settle(sendb.at[pl.ds(0, own - alone[tm_at] - counts[tm_at])], asend.at[0])
             settle(scales.at[pl.ds(0, groups)], ssend.at[0])
+            if tm_at in (0, n - 1):
+                settle(relayb.at[pl.ds(0, relay_runs(1 if tm_at == 0 else n - 2)[1])], fsend.at[0])
 
     sent = jnp.where(owns, NF - 1, NF)
     settle_count(gpart, sent, gsend.at[0], [NF - 1, NF])
@@ -587,6 +674,7 @@
             pltpu.VMEM((n, slots * ROWS, 3 * pw), f32),
             pltpu.VMEM((slots * n, ROWS, 3 * pw), jnp.int16),
             pltpu.VMEM((slots * n, ROWS, 3 * pw), jnp.int16),
+            pltpu.VMEM((slots * n // 2, ROWS, 3 * pw), bf16),
             pltpu.VMEM((n, slots, 128), f32),
             pltpu.VMEM((n, slots, 128), f32),
             pltpu.VMEM((slots * n, ROWS, 3 * pw), bf16),
@@ -596,7 +684,7 @@
             pltpu.VMEM((total, NB // 4, 4 * NB), f32),
             pltpu.VMEM((NB // 2, 4 * NB), bf16),
             pltpu.VMEM((NF, NB // 2, 4 * NB), bf16),
-            dma((1 + n // 2,)), dma((1,)), dma((n,)), dma((1,)), dma((n,)),
+            dma((1 + n // 2,)), dma((1,)), dma((n,)), dma((1,)), dma((1,)), dma((1,)), dma((n,)),
             dma((1,)), dma((1,)), dma((1,)), dma((1,)), dma((1,)), dma((1,)),
         ],
         compiler_params=pltpu.CompilerParams(

time: 44 us -> 41.9 us (0.952)
  Pallas kernels: 42.5 us -> 40.4 us
    pallas_call x1, Pallas kernels: 41.2 us -> 39.1 us  [fused(): pl.pallas_call(functools.partial(kernel, n, nf_dev, per, whole, shared, h...]
where the time goes in v6:
time: 41.9 us; the launch traced here: 41.8 us
  Pallas kernels  40.4 us (96%)
  other arithmetic  0.75 us (2%)
  between operations  0.64 us (2%)
    pallas_call x1, Pallas kernels, fused(): pl.pallas_call(functools.partial(kernel, n, nf_dev, per, whole, shared, h...  39.1 us
    pallas_call x1, Pallas kernels, fused(): pl.pallas_call(finish_kernel, out_shape=(jax.ShapeDtypeStruct((NF * NB *...  1.29 us

profile of v6, /device:TPU:0, one launch (start us, length us, event | category | flops | bytes accessed | tf_op | source)
XLA Modules:
  0.0 41.8 jit_solution(8600894889890896751)
XLA Ops:
  0.6 0.7 %pad_add_fusion.ints_hbm = s32[48]{0:T(128)S(1)} fusion(s32[16]{0:T(128)} %param.5, s32[32]{0:T(128)} %param.4), kind=kLoop, calls=%fused_computation | loop fusion | flops 48 | bytes 384 | tf_op jit(solution)/shard_map/concatenate | solution.py:692
  1.4 39.1 %shard_map.50 = (bf16[16,64,384]{2,1,0:T(8,128)(2,1)S(1)}, bf16[16,16,128]{2,1,0:T(8,128)(2,1)S(1)}) custom-call(bf16[3,544,1024]{2,1,0:T(8,128)(2,1)} %bitcast.5, s32[48]{0:T(128)S(1)} %pad_add_fusion.ints_hbm), custom_call_target="tpu_custom_call" | custom-call | tf_op jit(solution)/shard_map/pallas_call | solution.py:664
  40.5 1.3 %shard_map.51 = (bf16[3072,128]{1,0:T(8,128)(2,1)}, f32[1,16]{1,0:T(1,128)}) custom-call(bf16[16,64,384]{2,1,0:T(8,128)(2,1)S(1)} %get-tuple-element.6.spec, bf16[16,16,128]{2,1,0:T(8,128)(2,1)S(1)} %get-tuple-element.7.crecv), custom_call_target="tpu_custom_call" | custom-call | tf_op jit(solution)/shard_map/pallas_call | solution.py:693

commit v7 on v6

--- a/solution.py
+++ b/solution.py
@@ -405,16 +405,16 @@
             for d in range(2):
                 parts[2 * g + d, :, c * pw : (c + 1) * pw] = part[:, d * pw : (d + 1) * pw]
 
-        @pl.when(k == 0)
-        def _():
-            pl.semaphore_wait(barrier, total - 1)
-
         for d in range(2):
             for slot in range(slots):
                 if shared[slot]:
                     @pl.when(member(tm, shared[slot]) & is_theirs(slot, 2 * g + d))
                     def _(slot=slot, d=d):
                         encode(slot, g, d)
+
+        @pl.when(k == 0)
+        def _():
+            pl.semaphore_wait(barrier, total - 1)
 
         for side in range(2):
             _, whole_group, all_mine = division(n, tm, side, 2 * g)

time: 41.9 us -> 41 us (0.979)
  Pallas kernels: 40.4 us -> 39.5 us
    pallas_call x1, Pallas kernels: 39.1 us -> 38.2 us  [fused(): pl.pallas_call(functools.partial(kernel, n, nf_dev, per, whole, shared, h...]
where the time goes in v7:
time: 41 us; the launch traced here: 40.9 us
  Pallas kernels  39.5 us (96%)
  other arithmetic  0.75 us (2%)
  between operations  0.64 us (2%)
    pallas_call x1, Pallas kernels, fused(): pl.pallas_call(functools.partial(kernel, n, nf_dev, per, whole, shared, h...  38.2 us
    pallas_call x1, Pallas kernels, fused(): pl.pallas_call(finish_kernel, out_shape=(jax.ShapeDtypeStruct((NF * NB *...  1.29 us

profile of v7, /device:TPU:0, one launch (start us, length us, event | category | flops | bytes accessed | tf_op | source)
XLA Modules:
  0.0 40.9 jit_solution(17317684825535605347)
XLA Ops:
  0.6 0.7 %pad_add_fusion.ints_hbm = s32[48]{0:T(128)S(1)} fusion(s32[16]{0:T(128)} %param.5, s32[32]{0:T(128)} %param.4), kind=kLoop, calls=%fused_computation | loop fusion | flops 48 | bytes 384 | tf_op jit(solution)/shard_map/concatenate | solution.py:692
  1.4 38.2 %shard_map.50 = (bf16[16,64,384]{2,1,0:T(8,128)(2,1)S(1)}, bf16[16,16,128]{2,1,0:T(8,128)(2,1)S(1)}) custom-call(bf16[3,544,1024]{2,1,0:T(8,128)(2,1)} %bitcast.5, s32[48]{0:T(128)S(1)} %pad_add_fusion.ints_hbm), custom_call_target="tpu_custom_call" | custom-call | tf_op jit(solution)/shard_map/pallas_call | solution.py:664
  39.6 1.3 %shard_map.51 = (bf16[3072,128]{1,0:T(8,128)(2,1)}, f32[1,16]{1,0:T(1,128)}) custom-call(bf16[16,64,384]{2,1,0:T(8,128)(2,1)S(1)} %get-tuple-element.6.spec, bf16[16,16,128]{2,1,0:T(8,128)(2,1)S(1)} %get-tuple-element.7.crecv), custom_call_target="tpu_custom_call" | custom-call | tf_op jit(solution)/shard_map/pallas_call | solution.py:693

commit v8 on v7

--- a/solution.py
+++ b/solution.py
@@ -211,6 +211,8 @@
                 "freq": jnp.where(col >= nf_dev, col - nf_dev, col)}
 
     def group(k):
+        inner = (tm // 2 > 0) & (tm // 2 < half_n - 1) & (k >= half_n - 2)
+        k = jnp.where(inner, 2 * half_n - 3 - k, k)
         return jnp.where(tm < half_n, half_n - 1 - k, k)
 
     def load(g, c):
@@ -276,7 +278,7 @@
         block = per * tm + slot - 2
         return pltpu.make_async_remote_copy(
             src_ref=sendb.at[pl.ds(dest * slots + slot, length)], dst_ref=recvb.at[pl.ds(block, length)],
-            send_sem=asend.at[0], recv_sem=arecv.at[0],
+            send_sem=asend.at[0], recv_sem=arecv.at[jnp.where(block > NB // 2, 1, 0)],
             device_id={"tm": dest, "freq": fr}, device_id_type=MESH)
 
     def settle(ref, sem):
@@ -367,7 +369,7 @@
                         pltpu.make_async_remote_copy(
                             src_ref=relayb.at[pl.ds(spot, length)],
                             dst_ref=recvb.at[pl.ds(per * source + first - 2, length)],
-                            send_sem=fsend.at[0], recv_sem=arecv.at[0],
+                            send_sem=fsend.at[0], recv_sem=arecv.at[int(per * source + first - 2 > NB // 2)],
                             device_id={"tm": dest, "freq": fr}, device_id_type=MESH).start()
 
     def send_whole(dest, chosen):
@@ -490,17 +492,26 @@
 
     alone = [sum(tm_at in devs for devs in whole) for tm_at in range(n)]
     pitch = spec32.shape[1] // NB
-    missing = [NB - alone[tm_at] - counts[tm_at] for tm_at in range(n)]
-    settle_count(recvb, sum(jnp.where(tm == tm_at, missing[tm_at], 0) for tm_at in range(n)), arecv.at[0], missing)
+    late = []
     for block in range(NB):
-        values = recvb[block]
-        for c in range(3):
-            spec32[c, block * pitch : block * pitch + ROWS, :] = values[:, c * 128 : (c + 1) * 128].astype(jnp.float32)
-    for f in range(NF):
-        for r in range(2):
-            spec[f, r * NB : (r + 1) * NB, :] = jnp.concatenate([
-                spec32[c, pl.ds(2 * f + r, NB, stride=pitch), :].astype(jnp.bfloat16)
-                for c in range(3)], axis=1)
+        first = block
+        while first and holders[first - 1] == holders[block]:
+            first -= 1
+        late.append(int(first > NB // 2))
+    for h in range(2):
+        group_of = [block for block in range(NB) if late[block] == h]
+        missing = [sum(tm_at not in holders[block] for block in group_of) for tm_at in range(n)]
+        settle_count(recvb, sum(jnp.where(tm == tm_at, missing[tm_at], 0) for tm_at in range(n)), arecv.at[h], missing)
+        for block in group_of:
+            values = recvb[block]
+            for c in range(3):
+                spec32[c, block * pitch : block * pitch + ROWS, :] = values[:, c * 128 : (c + 1) * 128].astype(jnp.float32)
+        low_row = h * NB // 2
+        for f in range(NF):
+            for r in range(2):
+                spec[f, r * NB + low_row : r * NB + low_row + NB // 2, :] = jnp.concatenate([
+                    spec32[c, pl.ds(low_row * pitch + 2 * f + r, NB // 2, stride=pitch), :].astype(jnp.bfloat16)
+                    for c in range(3)], axis=1)
 
     def to_owner(k):
         first, last = owner(NF - 1 - k), owner(k)
@@ -685,7 +696,7 @@
             pltpu.VMEM((NB // 2, 4 * NB), bf16),
             pltpu.VMEM((NF, NB // 2, 4 * NB), bf16),
             dma((1 + n // 2,)), dma((1,)), dma((n,)), dma((1,)), dma((1,)), dma((1,)), dma((n,)),
-            dma((1,)), dma((1,)), dma((1,)), dma((1,)), dma((1,)), dma((1,)),
+            dma((1,)), dma((2,)), dma((1,)), dma((1,)), dma((1,)), dma((1,)),
         ],
         compiler_params=pltpu.CompilerParams(
             collective_id=0, has_side_effects=True, vmem_limit_bytes=54_000_000),

time: 41 us -> 41.1 us (level)
  no operation moved by 1% of the time
where the time goes in v8:
time: 41.1 us; the launch traced here: 41 us
  Pallas kernels  39.6 us (96%)
  other arithmetic  0.75 us (2%)
  between operations  0.64 us (2%)
    pallas_call x1, Pallas kernels, fused(): pl.pallas_call(functools.partial(kernel, n, nf_dev, per, whole, shared, h...  38.3 us
    pallas_call x1, Pallas kernels, fused(): pl.pallas_call(finish_kernel, out_shape=(jax.ShapeDtypeStruct((NF * NB *...  1.29 us

profile of v8, /device:TPU:0, one launch (start us, length us, event | category | flops | bytes accessed | tf_op | source)
XLA Modules:
  0.0 41.0 jit_solution(4958286423241888954)
XLA Ops:
  0.6 0.7 %pad_add_fusion.ints_hbm = s32[48]{0:T(128)S(1)} fusion(s32[16]{0:T(128)} %param.5, s32[32]{0:T(128)} %param.4), kind=kLoop, calls=%fused_computation | loop fusion | flops 48 | bytes 384 | tf_op jit(solution)/shard_map/concatenate | solution.py:703
  1.4 38.3 %shard_map.50 = (bf16[16,64,384]{2,1,0:T(8,128)(2,1)S(1)}, bf16[16,16,128]{2,1,0:T(8,128)(2,1)S(1)}) custom-call(bf16[3,544,1024]{2,1,0:T(8,128)(2,1)} %bitcast.5, s32[48]{0:T(128)S(1)} %pad_add_fusion.ints_hbm), custom_call_target="tpu_custom_call" | custom-call | tf_op jit(solution)/shard_map/pallas_call | solution.py:675
  39.7 1.3 %shard_map.51 = (bf16[3072,128]{1,0:T(8,128)(2,1)}, f32[1,16]{1,0:T(1,128)}) custom-call(bf16[16,64,384]{2,1,0:T(8,128)(2,1)S(1)} %get-tuple-element.6.spec, bf16[16,16,128]{2,1,0:T(8,128)(2,1)S(1)} %get-tuple-element.7.crecv), custom_call_target="tpu_custom_call" | custom-call | tf_op jit(solution)/shard_map/pallas_call | solution.py:704

commit v9 on v7

--- a/solution.py
+++ b/solution.py
@@ -628,13 +628,13 @@
     lanes = lax.broadcasted_iota(jnp.int32, (NB, 2 * NB), 1)
     signs = jnp.where(lanes < NB, 1.0, -1.0).astype(jnp.bfloat16)
     hidden = lanes == NB + lax.broadcasted_iota(jnp.int32, (NB, 2 * NB), 0)
-    wide_lane = lax.broadcasted_iota(jnp.int32, (1, NF), 1)
-    energies = jnp.zeros((1, NF), jnp.float32)
+    tall_row = lax.broadcasted_iota(jnp.int32, (NF, 2 * NB), 0)
+    energies = jnp.zeros((NF, 2 * NB), jnp.float32)
     for f in range(NF):
         pairs = crecv[f]
         straight = jnp.concatenate([pairs[:, : 2 * NB], pairs[:, 2 * NB :]], axis=0)
-        found = jnp.sum(jnp.where(hidden, straight.astype(jnp.float32), 0.0), axis=(0, 1), keepdims=True)
-        energies = jnp.where(wide_lane == f, found, energies)
+        found = jnp.sum(jnp.where(hidden, straight.astype(jnp.float32), 0.0), axis=0, keepdims=True)
+        energies = jnp.where(tall_row == f, found, energies)
         straight = jnp.where(hidden, jnp.zeros_like(straight), straight)
         crossed = jnp.concatenate([straight[:, NB:], straight[:, :NB]], axis=1)
         stacked = jnp.concatenate([straight * signs, crossed], axis=0)
@@ -645,7 +645,9 @@
         modes_ref[f * 6 * NB : (f + 1) * 6 * NB, :] = stage[f % 4].astype(jnp.bfloat16)
         part = pl.ds(f * 6 * NB, 6 * NB)
         pltpu.make_async_copy(modes_ref.at[part], modes_hbm.at[part], sem.at[0]).start()
-    energy_ref[...] = energies
+    column = jnp.sum(energies, axis=1, keepdims=True)
+    square = lax.broadcasted_iota(jnp.int32, (NF, NF), 0) == lax.broadcasted_iota(jnp.int32, (NF, NF), 1)
+    energy_ref[...] = jnp.sum(jnp.where(square, column, 0.0), axis=0, keepdims=True)
     last = pltpu.make_async_copy(energy_ref, energy_hbm, sem.at[1])
     last.start()
     pltpu.make_async_copy(modes_ref, modes_hbm, sem.at[0]).wait()

time: 41 us -> 41 us (level)
  no operation moved by 1% of the time
where the time goes in v9:
time: 41 us; the launch traced here: 40.9 us
  Pallas kernels  39.5 us (96%)
  other arithmetic  0.75 us (2%)
  between operations  0.64 us (2%)
    pallas_call x1, Pallas kernels, fused(): pl.pallas_call(functools.partial(kernel, n, nf_dev, per, whole, shared, h...  38.2 us
    pallas_call x1, Pallas kernels, fused(): pl.pallas_call(finish_kernel, out_shape=(jax.ShapeDtypeStruct((NF * NB *...  1.29 us

profile of v9, /device:TPU:0, one launch (start us, length us, event | category | flops | bytes accessed | tf_op | source)
XLA Modules:
  0.0 40.9 jit_solution(5576572841759673744)
XLA Ops:
  0.6 0.7 %pad_add_fusion.ints_hbm = s32[48]{0:T(128)S(1)} fusion(s32[16]{0:T(128)} %param.5, s32[32]{0:T(128)} %param.4), kind=kLoop, calls=%fused_computation | loop fusion | flops 48 | bytes 384 | tf_op jit(solution)/shard_map/concatenate | solution.py:694
  1.4 38.2 %shard_map.50 = (bf16[16,64,384]{2,1,0:T(8,128)(2,1)S(1)}, bf16[16,16,128]{2,1,0:T(8,128)(2,1)S(1)}) custom-call(bf16[3,544,1024]{2,1,0:T(8,128)(2,1)} %bitcast.5, s32[48]{0:T(128)S(1)} %pad_add_fusion.ints_hbm), custom_call_target="tpu_custom_call" | custom-call | tf_op jit(solution)/shard_map/pallas_call | solution.py:666
  39.6 1.3 %shard_map.51 = (bf16[3072,128]{1,0:T(8,128)(2,1)}, f32[1,16]{1,0:T(1,128)}) custom-call(bf16[16,64,384]{2,1,0:T(8,128)(2,1)S(1)} %get-tuple-element.6.spec, bf16[16,16,128]{2,1,0:T(8,128)(2,1)S(1)} %get-tuple-element.7.crecv), custom_call_target="tpu_custom_call" | custom-call | tf_op jit(solution)/shard_map/pallas_call | solution.py:695
